TPU v7x, 32 devices: a whole 2x2x4 slice. The times are simulated.
32 devices in a mesh: dp: 8 (over z, y), mp: 4 (over x, core).
Axes of the slice: x: 2, y: 2, z: 4, core: 2. Of those that a mesh axis runs over, the one named last changes fastest.
Arguments:
- noise_blocks: bfloat16 [64, 12800], P('dp'), may hold values from -6 to 6
- data_blocks: bfloat16 [64, 12800], P('dp'), may hold values from -6 to 6
- destination: int32 [64], replicated, may hold values from 0 to 63, as said below
- utt_blocks: int32 [8, 4], P('dp'), may hold values from 1 to 4, 8 in all within a row
- span_start: int32 [8, 4], P('dp'), may hold values from 0 to 19
- span_size: int32 [8, 4], P('dp'), may hold values from 44 to 64
- timestep: int32 [8, 4], P('dp'), may hold values from 1 to 63
- in_weight: bfloat16 [200, 1024], replicated, may hold values from -0.4375 to 0.4375
- norm_gain: bfloat16 [1024], replicated, may hold values from 0.5 to 1.5
- qkv_weight: bfloat16 [1024, 3, 512], P(None, None, 'mp'), may hold values from -4 to 4
- out_proj: bfloat16 [512, 1024], P('mp'), may hold values from -0.25 to 0.25
- final_gain: bfloat16 [1024], replicated, may hold values from 0.25 to 1.75
- vel_weight: bfloat16 [1024, 100], replicated, may hold values from -0.1875 to 0.1875
Outputs:
- grad_qkv: float32 [1024, 3, 512], P('dp', None, 'mp')
- grad_out: float32 [512, 1024], P('mp', 'dp')
Inputs may be any that keep to these rules, and one draw needn't show every extreme that they name: `destination`: A permutation of the 64 bin positions; a device sends to each bin either none or exactly 1 of its blocks.
All inputs are finite; a program needn't handle non-finite values.
Results may differ from a plain program's by a relative error of at most 0.004.
Values may be sent and summed in bfloat16 or wider, within the bound.
A program may use at most 64 MiB of HBM per device.

v0:
```python
import functools

import jax
import jax.numpy as jnp
from jax import lax
from jax.experimental import pallas as pl
from jax.experimental.pallas import tpu as pltpu
from jax.sharding import PartitionSpec as P

HEAD_DIM = 64
BLOCK = 128
MESH = pl.DeviceIdType.MESH
VMEM = pl.BlockSpec(memory_space=pltpu.VMEM)
SMEM = pl.BlockSpec(memory_space=pltpu.SMEM)
F32, BF16 = jnp.float32, jnp.bfloat16
NT = (((1,), (1,)), ((), ()))
TN = (((0,), (0,)), ((), ()))


def dot(a, b, dims=(((1,), (0,)), ((), ()))):
    return lax.dot_general(a, b, dims, preferred_element_type=F32)


def params(**kw):
    return pltpu.CompilerParams(vmem_limit_bytes=56 * 2**20, **kw)


def greet(dp, mp, with_dp, with_mp):
    me, my = lax.axis_index("dp"), lax.axis_index("mp")
    barrier = pltpu.get_barrier_semaphore()
    n = 0
    if with_dp:
        for i in range(1, dp):
            pl.semaphore_signal(
                barrier, inc=1, device_id=(lax.rem(me + i, dp), my), device_id_type=MESH
            )
        n += dp - 1
    if with_mp:
        for i in range(1, mp):
            pl.semaphore_signal(
                barrier, inc=1, device_id=(me, lax.rem(my + i, mp)), device_id_type=MESH
            )
        n += mp - 1
    return lambda: pl.semaphore_wait(barrier, n)


PIECES = 4


def gather_mp(mp, src_at, dst_at, local, send, recv, fsend, frecv):
    me, my = lax.axis_index("dp"), lax.axis_index("mp")
    pair, side = my // 2, lax.rem(my, 2)
    mate = pair * 2 + 1 - side
    direct, keep, near = [], [], []
    for p in range(PIECES):
        keep.append(pltpu.make_async_copy(src_at(p), dst_at(my, p), local.at[p]))
        for c in range(1, mp // 2):
            far = lax.rem(pair + c, mp // 2) * 2 + side
            direct.append((p, c, pltpu.make_async_remote_copy(
                src_at(p), dst_at(my, p), send.at[c, p], recv.at[c, p],
                device_id=(me, far), device_id_type=MESH,
            )))
        near.append(pltpu.make_async_remote_copy(
            src_at(p), dst_at(my, p), send.at[0, p], recv.at[0, p],
            device_id=(me, mate), device_id_type=MESH,
        ))

    def start():
        for _, _, d in direct:
            d.start()
        for n in near + keep:
            n.start()

    def finish():
        onward = []
        for p, c, d in direct:
            d.wait_recv()
            origin = lax.rem(pair + mp // 2 - c, mp // 2) * 2 + side
            f = pltpu.make_async_remote_copy(
                dst_at(origin, p), dst_at(origin, p), fsend.at[c, p], frecv.at[c, p],
                device_id=(me, mate), device_id_type=MESH,
            )
            f.start()
            onward.append(f)
        for n in near + keep:
            n.wait()
        for _, _, d in direct:
            d.wait_send()
        for f in onward:
            f.wait()

    return start, finish


def load_kernel(
    dp, mp, dest_ref, utt_ref, start_ref, size_ref, x_ref, w_ref,
    bin_ref, full_ref, count_ref,
    stage, got, tally, send, recv, csend, crecv, hsend, hrecv, local, ssend, srecv, fsend, frecv,
):
    me, my = lax.axis_index("dp"), lax.axis_index("mp")
    wait = greet(dp, mp, True, True)
    per_dev = bin_ref.shape[1]
    owners = [dest_ref[me * per_dev + k] // per_dev for k in range(per_dev)]
    for i in range(dp):
        to = lax.rem(me + i, dp)
        pick = jnp.int32(0)
        for k in range(per_dev):
            pick = jnp.where(owners[k] == to, k, pick)
        for part in range(2):
            stage[i, part] = x_ref[part, pick]
    count = jnp.int32(0)
    for u in range(utt_ref.shape[1]):
        low = start_ref[0, u]
        high = jnp.minimum(low + size_ref[0, u], 64)
        count += (high - low) * utt_ref[0, u] * (BLOCK // 64)
    tally[me] = jnp.full(tally.shape[1:], count, jnp.int32).astype(F32)
    side = lax.rem(my, 2)
    mate = my + 1 - 2 * side
    half = BLOCK // 2
    lines = pl.ds(pl.multiple_of(side * half, half), half)
    got[me, :, lines] = stage[0, :, lines]
    wait()
    rows = w_ref.shape[0]
    piece = rows // PIECES
    start, finish = gather_mp(
        mp, lambda p: w_ref.at[pl.ds(p * piece, piece)],
        lambda i, p: full_ref.at[pl.ds(pl.multiple_of(i * rows + p * piece, piece), piece)],
        local, ssend, srecv, fsend, frecv,
    )
    frames, counts = [], []
    for i in range(1, dp):
        to = lax.rem(me + i, dp)
        frames.append(
            pltpu.make_async_remote_copy(
                stage.at[i, :, lines], got.at[me, :, lines], send.at[i], recv.at[i],
                device_id=(to, my), device_id_type=MESH,
            )
        )
        counts.append(
            pltpu.make_async_remote_copy(
                tally.at[me], tally.at[me], csend.at[i], crecv.at[i],
                device_id=(to, my), device_id_type=MESH,
            )
        )
    for c in frames + counts:
        c.start()
    start()
    onward = []
    for i in range(dp):
        if i > 0:
            frames[i - 1].wait_recv()
        slot = lax.rem(me + dp - i, dp)
        f = pltpu.make_async_remote_copy(
            got.at[slot, :, lines], got.at[slot, :, lines], hsend.at[i], hrecv.at[i],
            device_id=(me, mate), device_id_type=MESH,
        )
        f.start()
        onward.append(f)

    def find(i, found):
        d = dest_ref[i]
        return tuple(jnp.where(d == me * per_dev + j, i // per_dev, o) for j, o in enumerate(found))

    origin = lax.fori_loop(0, dp * per_dev, find, (jnp.int32(0),) * per_dev)
    finish()
    for c in frames:
        c.wait_send()
    for c in counts + onward:
        c.wait()
    for j in range(per_dev):
        for part in range(2):
            bin_ref[part, j] = got[origin[j], part]
    count_ref[...] = jnp.sum(tally[...], axis=0)


def gather_kernel(dp, mp, a_ref, out_ref, local, send, recv, fsend, frecv):
    greet(dp, mp, False, True)()
    piece = a_ref.shape[0] // PIECES
    start, finish = gather_mp(
        mp, lambda p: a_ref.at[pl.ds(p * piece, piece)],
        lambda i, p: out_ref.at[i, pl.ds(p * piece, piece)], local, send, recv, fsend, frecv,
    )
    start()
    finish()


def reduce_kernel(
    dp, mp, normed_ref, d_ref, back_ref, att_ref, count_ref, qkv_out, o_out,
    terms, near, sums, far, s1, r1, s2, r2,
):
    me, my = lax.axis_index("dp"), lax.axis_index("mp")
    ready = greet(dp, mp, True, False)
    rows, chunks, groups = o_out.shape[0], terms.shape[0], dp // 2
    group, side = me // 2, lax.rem(me, 2)
    mate = me + 1 - 2 * side
    width = o_out.shape[1]

    def block(j, g, s):
        return terms.at[j, pl.ds(pl.multiple_of((g * 2 + s) * rows, rows), rows)]

    first, second = [], []

    def middle(j):
        for i in range(1, groups):
            g = lax.rem(group + i, groups)
            first[j][i].wait_recv()
            sums[j, i] = (block(j, g, side)[...].astype(F32) + near[j, g].astype(F32)).astype(BF16)
            c = pltpu.make_async_remote_copy(
                sums.at[j, i], far.at[j, i], s2.at[j, i], r2.at[j, i],
                device_id=(g * 2 + side, my), device_id_type=MESH,
            )
            c.start()
            second.append(c)
        first[j][0].wait_recv()

    def last(j):
        total = block(j, group, side)[...].astype(F32) + near[j, group].astype(F32)
        for i in range(1, groups):
            second[j * (groups - 1) + i - 1].wait_recv()
            total += far[j, i].astype(F32)
        total = total / count_ref[0:1, :]
        if j == 0:
            o_out[...] = total.T if o_out.shape[0] == width else total
        else:
            qkv_out[j - 1] = total

    for j in range(chunks):
        if j == 0:
            t = dot(att_ref[...], back_ref[...], TN).T
        else:
            t = dot(d_ref[:, (j - 1) * width : j * width], normed_ref[...], TN).T
        terms[j] = t.astype(BF16)
        if j == 0:
            ready()
        out = []
        for i in range(groups):
            g = lax.rem(group + i, groups)
            out.append(
                pltpu.make_async_remote_copy(
                    block(j, g, 1 - side), near.at[j, g], s1.at[j, i], r1.at[j, i],
                    device_id=(mate, my), device_id_type=MESH,
                )
            )
        for c in out[1:] + out[:1]:
            c.start()
        first.append(out)
        if j > 0:
            middle(j - 1)
    middle(chunks - 1)
    for j in range(chunks):
        last(j)
    for out in first:
        for c in out:
            c.wait_send()
    for c in second:
        c.wait_send()


def utterances(utt_ref, longest, body):
    def step(u, at):
        length = utt_ref[0, u]
        for n in range(1, longest + 1):
            @pl.when(length == n)
            def _():
                body(pl.ds(pl.multiple_of(at * BLOCK, BLOCK), n * BLOCK))
        return at + length

    lax.fori_loop(0, utt_ref.shape[1], step, jnp.int32(0))


def span_table(utt_ref, start_ref, size_ref, step_ref, b):
    at = jnp.int32(0)
    offset = low = high = step = jnp.int32(0)
    for u in range(utt_ref.shape[1]):
        n = utt_ref[0, u]
        inside = (b >= at) & (b < at + n)
        lo = start_ref[0, u] * n * (BLOCK // 64)
        hi = (start_ref[0, u] + size_ref[0, u]) * n * (BLOCK // 64)
        offset = jnp.where(inside, (b - at) * BLOCK, offset)
        low = jnp.where(inside, lo, low)
        high = jnp.where(inside, hi, high)
        if step_ref is not None:
            step = jnp.where(inside, step_ref[0, u], step)
        at = at + n
    frame = offset + lax.broadcasted_iota(jnp.int32, (BLOCK, 1), 0)
    masked = ((frame >= low) & (frame < high)).astype(F32)
    return masked, step


def head_masks(width):
    lane = lax.broadcasted_iota(jnp.int32, (1, width), 1) // HEAD_DIM
    return [lane == h for h in range(width // HEAD_DIM)]


def softmax(s):
    e = jnp.exp(s - jnp.max(s, axis=1, keepdims=True))
    return e / jnp.sum(e, axis=1, keepdims=True)


def forward_kernel(
    longest, utt_ref, start_ref, size_ref, step_ref, bin_ref, win_ref, gain_ref, wqkv_ref,
    hidden_ref, normed_ref, qkv_ref, att_ref,
):
    width = att_ref.shape[1]
    gain = gain_ref[...].astype(F32).reshape(1, -1)

    def block(b, _):
        rows = pl.ds(pl.multiple_of(b * BLOCK, BLOCK), BLOCK)
        masked, step = span_table(utt_ref, start_ref, size_ref, step_ref, b)
        noise, data = bin_ref[0, b].astype(F32), bin_ref[1, b].astype(F32)
        level = jnp.full((1, 1), step, jnp.int32).astype(F32) / 64.0
        noisy = (1.0 - level) * noise + level * data
        cond = data * (1.0 - masked)
        inputs = jnp.concatenate([noisy, cond], axis=1).astype(BF16)
        hidden = dot(inputs, win_ref[...])
        hidden_ref[rows] = hidden
        scale = lax.rsqrt(jnp.mean(hidden * hidden, axis=1, keepdims=True) + 1e-06)
        normed = (hidden * scale * gain).astype(BF16)
        normed_ref[rows] = normed
        for j in range(3):
            qkv_ref[rows, j * width : (j + 1) * width] = dot(normed, wqkv_ref[j]).astype(BF16)
        return 0

    lax.fori_loop(0, bin_ref.shape[1], block, 0, unroll=2)
    masks = head_masks(width)

    def attend(rows):
        q = qkv_ref[rows, :width] * BF16(HEAD_DIM**-0.5)
        k, v = qkv_ref[rows, width : 2 * width], qkv_ref[rows, 2 * width :]
        out = None
        for m in masks:
            p = softmax(dot(jnp.where(m, q, BF16(0)), k, NT)).astype(BF16)
            o = dot(p, v)
            out = o if out is None else jnp.where(m, o, out)
        att_ref[rows] = out.astype(BF16)

    utterances(utt_ref, longest, attend)


def backward_kernel(
    longest, utt_ref, start_ref, size_ref, bin_ref, hidden_ref, all_ref, out_ref, own_ref, gain_ref,
    vel_ref, qkv_ref, back_ref, d_ref, do_ref,
):
    width = own_ref.shape[0]
    gain = gain_ref[...].astype(F32).reshape(1, -1)

    def block(b, _):
        rows = pl.ds(pl.multiple_of(b * BLOCK, BLOCK), BLOCK)
        masked, _ = span_table(utt_ref, start_ref, size_ref, None, b)
        mixed = None
        for g in range(all_ref.shape[0]):
            part = dot(all_ref[g, rows], out_ref[g * width : (g + 1) * width]).astype(BF16).astype(F32)
            mixed = part if mixed is None else mixed + part
        wide = (hidden_ref[rows] + mixed).astype(BF16).astype(F32)
        rscale = lax.rsqrt(jnp.mean(wide * wide, axis=1, keepdims=True) + 1e-06)
        normalized = wide * rscale
        velocity = dot((normalized * gain).astype(BF16), vel_ref[...], NT)
        target = bin_ref[1, b].astype(F32) - bin_ref[0, b].astype(F32)
        error = (2.0 * masked * (velocity - target)).astype(BF16)
        scaled = dot(error, vel_ref[...]) * gain
        back = (
            rscale * (scaled - normalized * jnp.mean(scaled * normalized, axis=1, keepdims=True))
        ).astype(BF16)
        back_ref[rows] = back
        do_ref[rows] = dot(back, own_ref[...], NT).astype(BF16)
        return 0

    lax.fori_loop(0, bin_ref.shape[1], block, 0, unroll=2)
    masks = head_masks(width)
    scale = HEAD_DIM**-0.5

    def pullback(rows):
        q = qkv_ref[rows, :width] * BF16(scale)
        k, v = qkv_ref[rows, width : 2 * width], qkv_ref[rows, 2 * width :]
        do = do_ref[rows]
        dq = dk = dv = None
        for m in masks:
            qh = jnp.where(m, q, BF16(0))
            doh = jnp.where(m, do, BF16(0))
            p = softmax(dot(qh, k, NT))
            dp = dot(doh, v, NT).astype(BF16).astype(F32)
            ds = (p * (dp - jnp.sum(dp * p, axis=1, keepdims=True))).astype(BF16)
            a, b, c = dot(ds, k), dot(ds, qh, TN), dot(p.astype(BF16), doh, TN)
            dq = a if dq is None else jnp.where(m, a, dq)
            dk = b if dk is None else dk + b
            dv = c if dv is None else dv + c
        d_ref[rows, :width] = (dq * scale).astype(BF16)
        d_ref[rows, width : 2 * width] = dk.astype(BF16)
        d_ref[rows, 2 * width :] = dv.astype(BF16)

    utterances(utt_ref, longest, pullback)


def shards(
    dp, mp, noise_blocks, data_blocks, destination, utt_blocks, span_start, span_size, timestep,
    in_weight, norm_gain, qkv_weight, out_proj, final_gain, vel_weight,
):
    per_dev = noise_blocks.shape[0]
    rows = per_dev * BLOCK
    mel = noise_blocks.shape[1] // BLOCK
    features = in_weight.shape[1]
    width = qkv_weight.shape[2]
    longest = min(4, per_dev)
    frames = jnp.concatenate([noise_blocks, data_blocks], axis=0).reshape(2, per_dev, BLOCK, mel)
    dma = pltpu.SemaphoreType.DMA

    def array(shape, kind):
        return jax.ShapeDtypeStruct(shape, kind)

    bins, out_full, count = pl.pallas_call(
        functools.partial(load_kernel, dp, mp),
        out_shape=(
            array(frames.shape, BF16), array((mp * width, features), BF16), array((8, 128), F32),
        ),
        in_specs=[SMEM] * 4 + [VMEM] * 2,
        out_specs=(VMEM,) * 3,
        scratch_shapes=[
            pltpu.VMEM((dp, 2, BLOCK, mel), BF16),
            pltpu.VMEM((dp, 2, BLOCK, mel), BF16),
            pltpu.VMEM((dp, 8, 128), F32),
        ] + [dma((dp,))] * 6 + [dma((PIECES,))] + [dma((mp, PIECES))] * 4,
        compiler_params=params(collective_id=0, has_side_effects=True),
        name="load_blocks",
    )(destination, utt_blocks, span_start, span_size, frames, out_proj)
    hidden0, normed, qkv, attended = pl.pallas_call(
        functools.partial(forward_kernel, longest),
        out_shape=(
            array((rows, features), F32), array((rows, features), BF16),
            array((rows, 3 * width), BF16), array((rows, width), BF16),
        ),
        in_specs=[SMEM] * 4 + [VMEM] * 4,
        out_specs=(VMEM,) * 4,
        compiler_params=params(),
        name="forward",
    )(utt_blocks, span_start, span_size, timestep, bins, in_weight, norm_gain, qkv_weight.transpose(1, 0, 2))
    everyone = pl.pallas_call(
        functools.partial(gather_kernel, dp, mp),
        out_shape=array((mp, rows, width), BF16),
        in_specs=[VMEM],
        out_specs=VMEM,
        scratch_shapes=[dma((PIECES,))] + [dma((mp, PIECES))] * 4,
        compiler_params=params(collective_id=1, has_side_effects=True),
        name="gather_attended",
    )(attended)
    back1, grads = pl.pallas_call(
        functools.partial(backward_kernel, longest),
        out_shape=(array((rows, features), BF16), array((rows, 3 * width), BF16)),
        in_specs=[SMEM] * 3 + [VMEM] * 8,
        out_specs=(VMEM,) * 2,
        scratch_shapes=[pltpu.VMEM((rows, width), BF16)],
        compiler_params=params(),
        name="backward",
    )(
        utt_blocks, span_start, span_size, bins, hidden0, everyone, out_full, out_proj,
        final_gain, vel_weight.T, qkv,
    )
    share, groups = features // dp, dp // 2
    summed_qkv, summed_out = pl.pallas_call(
        functools.partial(reduce_kernel, dp, mp),
        out_shape=(array((3, share, width), F32), array((share, width), F32)),
        in_specs=[VMEM] * 5,
        out_specs=(VMEM,) * 2,
        scratch_shapes=[
            pltpu.VMEM((4, features, width), BF16),
            pltpu.VMEM((4, groups, share, width), BF16),
            pltpu.VMEM((4, groups, share, width), BF16),
            pltpu.VMEM((4, groups, share, width), BF16),
        ] + [dma((4, groups))] * 4,
        compiler_params=params(collective_id=2, has_side_effects=True),
        name="reduce_grads",
    )(normed, grads, back1, attended, count)
    return (
        summed_qkv.transpose(1, 0, 2),
        summed_out if share == width else summed_out.T,
    )


def solution(mesh):
    in_specs = (
        P("dp", None), P("dp", None), P(), P("dp", None), P("dp", None), P("dp", None),
        P("dp", None), P(), P(), P(None, None, "mp"), P("mp", None), P(), P(),
    )
    out_specs = (P("dp", None, "mp"), P("mp", "dp"))
    return jax.shard_map(
        functools.partial(shards, mesh.shape["dp"], mesh.shape["mp"]),
        mesh=mesh, in_specs=in_specs, out_specs=out_specs, check_vma=False,
    )
```

profile of v0, /device:TPU:0, one launch (start us, length us, event | category | flops | bytes accessed | tf_op | source)
XLA Modules:
  0.0 92.8 jit_solution(3835981913662065007)
XLA Ops:
  0.6 1.1 %pad_maximum_fusion = bf16[16,12800]{1,0:T(8,128)(2,1)S(1)} fusion(bf16[8,12800]{1,0:T(8,128)(2,1)} %param.14, bf16[8,12800]{1,0:T(8,128)(2,1)} %param.13), kind=kLoop, calls=%fused_computation | loop fusion | flops 819200 | bytes 819200 | tf_op jit(solution)/shard_map/concatenate | solution.py:404
  1.7 2.8 %reshape.7.x_ref = bf16[2,8,128,100]{3,2,1,0:T(8,128)(2,1)} reshape(bf16[16,12800]{1,0:T(8,128)(2,1)S(1)} %pad_maximum_fusion) | data formatting | bytes 819200 | tf_op jit(solution)/shard_map/reshape | solution.py:404
  4.5 17.9 %load_blocks.1 = (bf16[2,8,128,100]{3,2,1,0:T(8,128)(2,1)}, bf16[512,1024]{1,0:T(8,128)(2,1)}, f32[8,128]{1,0:T(8,128)}) custom-call(s32[64]{0:T(128)} %dest_ref.1, s32[1,4]{1,0:T(1,128)} %utt_ref.5, s32[1,4]{1,0:T(1,128)} %start_ref.5, s32[1,4]{1,0:T(1,128)} %size_ref.5, bf16[2,8,128,100]{3,2,1,0:T(8,128)(2,1)} %reshape.7.x_ref, bf16[128,1024]{1,0:T(8,128)(2,1)} %own_ref.1), custom_call_target="tpu_custom_call" | custom-call | tf_op jit(solution)/shard_map/load_blocks/pallas_call | solution.py:410
  22.4 12.9 %forward.1 = (f32[1024,1024]{1,0:T(8,128)}, bf16[1024,1024]{1,0:T(8,128)(2,1)}, bf16[1024,384]{1,0:T(8,128)(2,1)}, bf16[1024,128]{1,0:T(8,128)(2,1)}) custom-call(s32[1,4]{1,0:T(1,128)} %utt_ref.5, s32[1,4]{1,0:T(1,128)} %start_ref.5, s32[1,4]{1,0:T(1,128)} %size_ref.5, s32[1,4]{1,0:T(1,128)} %step_ref.1, ...), custom_call_target="tpu_custom_call" | custom-call | tf_op jit(solution)/shard_map/forward/pallas_call | solution.py:425
  35.3 12.0 %gather_attended.1.all_ref = bf16[4,1024,128]{2,1,0:T(8,128)(2,1)} custom-call(bf16[1024,128]{1,0:T(8,128)(2,1)} %get-tuple-element.16.a_ref.att_ref), custom_call_target="tpu_custom_call" | custom-call | tf_op jit(solution)/shard_map/gather_attended/pallas_call | solution.py:436
  47.3 20.0 %backward.1 = (bf16[1024,1024]{1,0:T(8,128)(2,1)}, bf16[1024,384]{1,0:T(8,128)(2,1)}) custom-call(s32[1,4]{1,0:T(1,128)} %utt_ref.5, s32[1,4]{1,0:T(1,128)} %start_ref.5, s32[1,4]{1,0:T(1,128)} %size_ref.5, bf16[2,8,128,100]{3,2,1,0:T(8,128)(2,1)} %get-tuple-element.13.bin_ref, f32[1024,1024]{1,0:T(8,128)} %get-tuple-element.15.hidden_ref, ...), custom_call_target="tpu_custom_call" | custom-call | tf_op jit(solution)/shard_map/backward/pallas_call | solution.py:445
  67.3 22.3 %reduce_grads.1 = (f32[3,128,128]{2,1,0:T(8,128)}, f32[128,128]{1,0:T(8,128)}) custom-call(bf16[1024,1024]{1,0:T(8,128)(2,1)} %get-tuple-element.14.normed_ref, bf16[1024,384]{1,0:T(8,128)(2,1)} %get-tuple-element.19.d_ref, bf16[1024,1024]{1,0:T(8,128)(2,1)} %get-tuple-element.20.back_ref, bf16[1024,128]{1,0:T(8,128)(2,1)} %get-tuple-element.16.a_ref.att_ref, ...), custom_call_target="tpu_custom_call" | custom-call | tf_op jit(solution)/shard_map/reduce_grads/pallas_call | solution.py:458
  89.7 1.6 %copy.17 = f32[128,3,128]{2,0,1:T(8,128)} copy(f32[128,3,128]{2,0,1:T(8,128)} %bitcast.5) | data formatting | bytes 393216
  91.3 1.5 %copy.18 = f32[128,128]{1,0:T(8,128)} copy(f32[128,128]{1,0:T(8,128)} %get-tuple-element.27) | data formatting | bytes 131072
where the time goes:
time: 93 us; the launch traced here: 92.8 us
  Pallas kernels  85.2 us (92%)
  local copies, waits for them, and re-layouts  5.85 us (6%)
  other arithmetic  1.06 us (1%)
    pallas_call x1, Pallas kernels, shards(): pl.pallas_call(functools.partial(reduce_kernel, dp, mp), out_shape=(array...  22.3 us
    pallas_call x1, Pallas kernels, shards(): pl.pallas_call(functools.partial(backward_kernel, longest), out_shape=(ar...  20 us
    pallas_call x1, Pallas kernels, shards(): pl.pallas_call(functools.partial(load_kernel, dp, mp), out_shape=(array(f...  17.9 us
    pallas_call x1, Pallas kernels, shards(): pl.pallas_call(functools.partial(forward_kernel, longest), out_shape=(arr...  12.9 us
    pallas_call x1, Pallas kernels, shards(): pl.pallas_call(functools.partial(gather_kernel, dp, mp), out_shape=array(...  12 us
    unnamed x2, local copies, waits for them, and re-layouts  3.09 us
    reshape x1, local copies, waits for them, and re-layouts, shards(): jnp.concatenate([noise_blocks, data_blocks], axis=0)  2.76 us

commit v1 on v0

v1 whole, which is shorter than its diff:
```python
import functools

import jax
import jax.numpy as jnp
from jax import lax
from jax.experimental import pallas as pl
from jax.experimental.pallas import tpu as pltpu
from jax.sharding import PartitionSpec as P

HEAD_DIM = 64
BLOCK = 128
LANES = 128
LONGEST = 4
MESH = pl.DeviceIdType.MESH
VMEM = pl.BlockSpec(memory_space=pltpu.VMEM)
SMEM = pl.BlockSpec(memory_space=pltpu.SMEM)
ANY = pl.BlockSpec(memory_space=pl.ANY)
F32, BF16, I32 = jnp.float32, jnp.bfloat16, jnp.int32
NN = (((1,), (0,)), ((), ()))
NT = (((1,), (1,)), ((), ()))
TN = (((0,), (0,)), ((), ()))


def dot(a, b, dims=NN):
    return lax.dot_general(a, b, dims, preferred_element_type=F32)


def params(**kw):
    return pltpu.CompilerParams(vmem_limit_bytes=56 * 2**20, **kw)


def greet(dp, mp):
    me, my = lax.axis_index("dp"), lax.axis_index("mp")
    barrier = pltpu.get_barrier_semaphore()
    for i in range(1, dp):
        pl.semaphore_signal(
            barrier, inc=1, device_id=(lax.rem(me + i, dp), my), device_id_type=MESH
        )
    for i in range(1, mp):
        pl.semaphore_signal(
            barrier, inc=1, device_id=(me, lax.rem(my + i, mp)), device_id_type=MESH
        )
    return lambda: pl.semaphore_wait(barrier, dp - 1 + mp - 1)


def remote(src, dst, send, recv, device):
    return pltpu.make_async_remote_copy(
        src, dst, send, recv, device_id=device, device_id_type=MESH
    )


PIECES = 2
SLOT_AT, POS, SOURCE, FIRST, LENGTH, LOW, HIGH, STEP = range(8)


def step_kernel(
    dp, mp,
    dest_ref, utt_ref, start_ref, size_ref, step_ref,
    x_hbm, win_hbm, gain_ref, wqkv_hbm, own_hbm, gain2_ref, vel_hbm,
    out_ref, out2_ref,
    x_ref, win_ref, wpad, wqkv, wcat, own_ref, vel_ref, lsem, tall_ref,
    stage, got, tally, tab, out_full,
    hid_ref, normed_ref, qkv_ref, p_ref, pb_ref, att_ref, all_ref, back_ref,
    dosend, do_rel, do_ref, ds_ref, dt_ref,
    okeep, osend, onear, osum, ofar,
    tkeep, tsend, tnear, tsum, tfar,
    ukeep, usend, unear, usum, ufar,
    fsend, frecv, csend, crecv, hsend, hrecv,
    wsend, wrecv, wfsend, wfrecv,
    asend, arecv, dsend, drecv, o1s, o1r, o2s, o2r,
    t1s, t1r, t2s, t2r, u1s, u1r, u2s, u2r,
):
    me, my = lax.axis_index("dp"), lax.axis_index("mp")
    slots = normed_ref.shape[0]
    features = normed_ref.shape[2]
    width = own_ref.shape[0]
    mel = x_ref.shape[3]
    share = slots // mp
    pair, side = my // 2, lax.rem(my, 2)
    pairs = mp // 2
    mate = pair * 2 + 1 - side
    group, half = me // 2, lax.rem(me, 2)
    groups = dp // 2
    partner = group * 2 + 1 - half
    aligned = dp == slots

    wait = greet(dp, mp)
    loads = [
        pltpu.make_async_copy(a, b, lsem.at[n]) for n, (a, b) in enumerate((
            (x_hbm, x_ref), (win_hbm, win_ref), (wqkv_hbm, wqkv), (own_hbm, own_ref), (vel_hbm, vel_ref),
        ))
    ]
    for c in loads:
        c.start()
    owners = [dest_ref[me * slots + k] // slots for k in range(slots)]
    stage[...] = jnp.zeros_like(stage)
    loads[0].wait()
    for i in range(dp):
        to = lax.rem(me + i, dp)
        pick = jnp.int32(0)
        for k in range(slots):
            pick = jnp.where(owners[k] == to, k, pick)
        for part in range(2):
            stage[i, part, :, 0:mel] = x_ref[part, pick]
    count = jnp.int32(0)
    for u in range(utt_ref.shape[1]):
        low = start_ref[0, u]
        high = jnp.minimum(low + size_ref[0, u], 64)
        count += (high - low) * utt_ref[0, u] * (BLOCK // 64)
    tally[0] = jnp.full(tally.shape[1:], count, I32).astype(F32)
    got[0] = stage[0]
    lines = pl.ds(pl.multiple_of(side * (BLOCK // 2), BLOCK // 2), BLOCK // 2)
    wait()

    def frame_copy(i):
        return remote(
            stage.at[i, :, lines], got.at[i, :, lines], fsend.at[i], frecv.at[i],
            (lax.rem(me + i, dp), my),
        )

    def onward(i):
        return remote(
            got.at[i, :, lines], got.at[i, :, lines], hsend.at[i], hrecv.at[i], (me, mate)
        )

    def count_copy(i):
        return remote(tally.at[0], tally.at[i], csend.at[i], crecv.at[i], (lax.rem(me + i, dp), my))

    order = sorted(range(1, dp), key=lambda i: -min(i, dp - i))
    for i in order:
        frame_copy(i).start()
    for i in order:
        count_copy(i).start()
    loads[3].wait()
    piece = width // PIECES

    def full_at(a, b, p):
        return out_full.at[a, b, pl.ds(p * piece, piece)]

    def device_at(a, b):
        return (me, lax.rem(pair + pairs - a, pairs) * 2 + lax.rem(side + b, 2))

    def mine(p):
        return own_ref.at[pl.ds(p * piece, piece)]

    across = [
        remote(mine(p), full_at(c, 0, p), wsend.at[c, p], wrecv.at[c, p], device_at(pairs - c, 0))
        for p in range(PIECES) for c in range(1, pairs)
    ]
    beside = [
        remote(mine(p), full_at(0, 1, p), wsend.at[0, p], wrecv.at[0, p], (me, mate))
        for p in range(PIECES)
    ]
    for c in across + beside:
        c.start()
    out_full[0, 0] = own_ref[...]

    def find(i, found):
        d = dest_ref[i]
        return tuple(jnp.where(d == me * slots + j, i // slots, o) for j, o in enumerate(found))

    origin = lax.fori_loop(0, dp * slots, find, (jnp.int32(0),) * slots)
    origin = [lax.rem(me + dp - o, dp) for o in origin]
    for s in range(slots):
        if aligned:
            tab[SLOT_AT, s] = origin[s]
            pos = jnp.int32(0)
            for j in range(slots):
                pos = jnp.where(origin[j] == s, j, pos)
        else:
            tab[SLOT_AT, s] = jnp.int32(s)
            tab[SOURCE, s] = origin[s]
            pos = jnp.int32(s)
        at = first = length = low = high = step = jnp.int32(0)
        for u in range(utt_ref.shape[1]):
            n = utt_ref[0, u]
            inside = (pos >= at) & (pos < at + n)
            first = jnp.where(inside, at, first)
            length = jnp.where(inside, n, length)
            low = jnp.where(inside, start_ref[0, u] * n * (BLOCK // 64), low)
            high = jnp.where(inside, (start_ref[0, u] + size_ref[0, u]) * n * (BLOCK // 64), high)
            step = jnp.where(inside, step_ref[0, u], step)
            at = at + n
        tab[POS, s] = pos
        tab[FIRST, s] = first
        tab[LENGTH, s] = length
        tab[LOW, s] = low
        tab[HIGH, s] = high
        tab[STEP, s] = step

    loads[1].wait()
    wpad[...] = jnp.zeros_like(wpad)
    wpad[0:mel] = win_ref[0:mel]
    wpad[LANES : LANES + mel] = win_ref[mel : 2 * mel]
    loads[2].wait()
    for j in range(3):
        wcat[:, j * width : (j + 1) * width] = wqkv[j]
    gain = gain_ref[...].astype(F32).reshape(1, -1)

    def masked_of(s):
        frame = (tab[POS, s] - tab[FIRST, s]) * BLOCK + lax.broadcasted_iota(I32, (BLOCK, 1), 0)
        return ((frame >= tab[LOW, s]) & (frame < tab[HIGH, s])).astype(F32)

    def inputs_of(s):
        src = s if aligned else tab[SOURCE, s]
        noise, data = got[src, 0].astype(F32), got[src, 1].astype(F32)
        level = jnp.full((1, 1), tab[STEP, s], I32).astype(F32) / 64.0
        noisy = (1.0 - level) * noise + level * data
        cond = data * (1.0 - masked_of(s))
        return jnp.concatenate([noisy, cond], axis=1).astype(BF16)

    def encode(pieces):
        hidden = dot(jnp.concatenate([inputs_of(s) for s in pieces], axis=0), wpad[...])
        scale = lax.rsqrt(jnp.mean(hidden * hidden, axis=1, keepdims=True) + 1e-06)
        normed = (hidden * scale * gain).astype(BF16)
        qkv = dot(normed, wcat[...]).astype(BF16)
        for n, s in enumerate(pieces):
            rows = slice(n * BLOCK, (n + 1) * BLOCK)
            hid_ref[s] = hidden[rows]
            normed_ref[s] = normed[rows]
            qkv_ref[s] = qkv[rows]

    def receive(pieces):
        for i in pieces:
            if i:
                frame_copy(i).wait_recv()
                onward(i).start()

    def settle(pieces):
        for i in pieces:
            if i:
                onward(i).wait_recv()

    near_first = [0] + order[::-1]
    rounds = [near_first[n : n + 2] for n in range(0, dp, 2)]
    if aligned:
        receive(rounds[0])
        for n, pieces in enumerate(rounds):
            if n + 1 < len(rounds):
                receive(rounds[n + 1])
            settle(pieces)
            encode(pieces)
    else:
        for pieces in rounds:
            receive(pieces)
        for pieces in rounds:
            settle(pieces)
        for n in range(0, slots, 2):
            encode([n, n + 1])

    passed = []
    for p in range(PIECES):
        for c in range(1, pairs):
            across[p * (pairs - 1) + c - 1].wait_recv()
            f = remote(full_at(c, 0, p), full_at(c, 1, p), wfsend.at[c, p], wfrecv.at[c, p], (me, mate))
            f.start()
            passed.append(f)

    window = min(LONGEST, slots)
    heads = width // HEAD_DIM
    lane = lax.broadcasted_iota(I32, (1, width), 1) // HEAD_DIM
    masks = [lane == h for h in range(heads)]

    def split(a):
        return jnp.concatenate([jnp.where(m, a, BF16(0)) for m in masks], axis=0)

    def merge(o):
        out = o[0:BLOCK]
        for h in range(1, heads):
            out = jnp.where(masks[h], o[h * BLOCK : (h + 1) * BLOCK], out)
        return out

    def window_of(s):
        begin = jnp.minimum(tab[FIRST, s], slots - window)
        at = [tab[SLOT_AT, begin + i] for i in range(window)]
        valid = [
            (begin + i >= tab[FIRST, s]) & (begin + i < tab[FIRST, s] + tab[LENGTH, s])
            for i in range(window)
        ]
        return begin, at, valid

    def query_of(s):
        return split(qkv_ref[s, :, 0:width] * BF16(HEAD_DIM**-0.5))

    def window_cols(at, j):
        return jnp.concatenate([qkv_ref[i, :, j * width : (j + 1) * width] for i in at], axis=0)

    def attend(s):
        _, at, valid = window_of(s)
        place = lax.broadcasted_iota(I32, (1, window * BLOCK), 1) // BLOCK
        bias = jnp.zeros((1, window * BLOCK), F32)
        for i in range(window):
            bias = jnp.where(place == i, jnp.where(valid[i], F32(0), F32(-1e30)), bias)
        scores = dot(query_of(s), window_cols(at, 1), NT) + bias
        e = jnp.exp(scores - jnp.max(scores, axis=1, keepdims=True))
        probs = e * (1.0 / jnp.sum(e, axis=1, keepdims=True))
        p_ref[s] = probs
        short = probs.astype(BF16)
        for i in range(window):
            pb_ref[s, i] = short[:, i * BLOCK : (i + 1) * BLOCK]
        return merge(dot(short, window_cols(at, 2))).astype(BF16)

    spots = [(a, b) for a in range(pairs - 1, -1, -1) for b in (1, 0)]
    others = spots[:-1]

    def first_slot(a, b):
        return device_at(a, b)[1] * share

    def att_copy(a, b, i):
        return remote(
            att_ref.at[a, b, i], all_ref.at[a, b, i], asend.at[a, b, i], arecv.at[a, b, i],
            device_at(pairs - a, b),
        )

    for a, b in others:
        for i in range(share):
            att_ref[a, b, i] = attend(first_slot(pairs - a, b) + i)
            att_copy(a, b, i).start()
    for i in range(share):
        all_ref[0, 0, i] = attend(my * share + i)
    for c in beside:
        c.wait_recv()
    for f in passed:
        f.wait_recv()
    loads[4].wait()
    gain2 = gain2_ref[...].astype(F32).reshape(1, -1)
    for a, b in others:
        for i in range(share):
            att_copy(a, b, i).wait_recv()
    full = jnp.concatenate([out_full[a, b] for a, b in spots], axis=0)

    def do_copy(a, b, i):
        back_a = (pairs - a) % pairs
        return remote(
            dosend.at[a, b, i], do_rel.at[back_a, b, i], dsend.at[a, b, i], drecv.at[back_a, b, i],
            device_at(a, b),
        )

    for i in range(share):
        s = my * share + i
        mixed = None
        for a, b in spots:
            part = dot(all_ref[a, b, i], out_full[a, b]).astype(BF16).astype(F32)
            mixed = part if mixed is None else mixed + part
        wide = (hid_ref[s] + mixed).astype(BF16).astype(F32)
        rscale = lax.rsqrt(jnp.mean(wide * wide, axis=1, keepdims=True) + 1e-06)
        normalized = wide * rscale
        velocity = dot((normalized * gain2).astype(BF16), vel_ref[...], NT)
        src = s if aligned else tab[SOURCE, s]
        target = (got[src, 1].astype(F32) - got[src, 0].astype(F32))[:, 0:mel]
        error = (2.0 * masked_of(s) * (velocity - target)).astype(BF16)
        scaled = dot(error, vel_ref[...]) * gain2
        back = (
            rscale * (scaled - normalized * jnp.mean(scaled * normalized, axis=1, keepdims=True))
        ).astype(BF16)
        back_ref[i] = back
        do = dot(back, full, NT).astype(BF16)
        for n, (a, b) in enumerate(spots):
            piece_do = do[:, n * width : (n + 1) * width]
            if (a, b) == (0, 0):
                do_ref[s] = piece_do
            else:
                dosend[a, b, i] = piece_do
                do_copy(a, b, i).start()

    back = jnp.concatenate([back_ref[i] for i in range(share)], axis=0)

    def out_term(a, b):
        return dot(jnp.concatenate([all_ref[a, b, i] for i in range(share)], axis=0), back, TN)

    def o_first(c):
        return remote(osend.at[c], onear.at[c], o1s.at[c], o1r.at[c], (me, mate))

    def o_second(c):
        return remote(osum.at[c], ofar.at[c], o2s.at[c], o2r.at[c], device_at(c, 0))

    for c in range(pairs - 1, -1, -1):
        osend[c] = out_term(c, 1).astype(BF16)
        o_first(c).start()
    for c in range(pairs):
        okeep[c] = out_term(c, 0)

    for u, (a, b) in enumerate(spots[::-1]):
        if u == 2:
            for c in range(1, pairs):
                o_first(c).wait_recv()
                osum[c] = (okeep[c] + onear[c].astype(F32)).astype(BF16)
                o_second(c).start()
        for i in range(share):
            s = first_slot(a, b) + i
            if u:
                do_copy((pairs - a) % pairs, b, i).wait_recv()
                do_ref[s] = do_rel[a, b, i]
        for i in range(share):
            s = first_slot(a, b) + i
            _, at, _ = window_of(s)
            probs = p_ref[s]
            dprobs = dot(split(do_ref[s]), window_cols(at, 2), NT).astype(BF16).astype(F32)
            ds = (probs * (dprobs - jnp.sum(dprobs * probs, axis=1, keepdims=True))).astype(BF16)
            for n in range(window):
                ds_ref[s, n] = ds[:, n * BLOCK : (n + 1) * BLOCK]
            dq = merge(dot(ds, window_cols(at, 1))) * (HEAD_DIM**-0.5)
            dt_ref[s, 0:width] = dq.T.astype(BF16)

    def keys_step(s, _):
        begin, at, valid = window_of(s)
        own = jnp.clip(tab[POS, s] - begin, 0, window - 1)

        def pick(ref):
            return jnp.concatenate(
                [jnp.where(valid[i], ref[at[i], own], BF16(0)) for i in range(window)], axis=0
            )

        queries = jnp.concatenate([query_of(i) for i in at], axis=0)
        couts = jnp.concatenate([split(do_ref[i]) for i in at], axis=0)
        dt_ref[s, width : 2 * width] = dot(queries, pick(ds_ref), TN).astype(BF16)
        dt_ref[s, 2 * width :] = dot(couts, pick(pb_ref), TN).astype(BF16)
        return 0

    lax.fori_loop(0, slots, keys_step, 0)

    d_all = jnp.concatenate([dt_ref[s] for s in range(slots)], axis=1)

    def t_first(i):
        return remote(tsend.at[i], tnear.at[i], t1s.at[i], t1r.at[i], (partner, my))

    def t_second(i):
        g = lax.rem(group + i, groups)
        return remote(tsum.at[i], tfar.at[i], t2s.at[i], t2r.at[i], (g * 2 + half, my))

    def u_first(i):
        return remote(usend.at[i], unear.at[i], u1s.at[i], u1r.at[i], (partner, my))

    def u_second(i):
        g = lax.rem(group + i, groups)
        return remote(usum.at[i], ufar.at[i], u2s.at[i], u2r.at[i], (g * 2 + half, my))

    cols = features // dp
    flat = cols % LANES == 0

    def columns(owner):
        return pl.ds(pl.multiple_of(owner * cols, cols), cols)

    if flat:
        def term(owner):
            normed = jnp.concatenate([normed_ref[s, :, columns(owner)] for s in range(slots)], axis=0)
            return dot(d_all, normed)
    else:
        normed_all = jnp.concatenate([normed_ref[s] for s in range(slots)], axis=0)
        for j in range(3):
            rows = d_all[j * width : (j + 1) * width]
            tall_ref[:, j * width : (j + 1) * width] = dot(rows, normed_all).T

        def term(owner):
            return tall_ref[columns(owner), 0 : 3 * width]

    far_first = sorted(range(1, groups), key=lambda i: -min(i, groups - i)) + [0]
    for i in far_first:
        g = lax.rem(group + i, groups)
        tsend[i] = term(g * 2 + 1 - half).astype(BF16)
        t_first(i).start()
        tkeep[i] = term(g * 2 + half)
    o_first(0).wait_recv()
    total = okeep[0] + onear[0].astype(F32)
    for c in range(1, pairs):
        o_second(c).wait_recv()
        total += ofar[c].astype(F32)
    if flat:
        okeep[0] = total
    else:
        tall_ref[:, 3 * width :] = total.T

    def out_piece(owner):
        return okeep[0, :, columns(owner)] if flat else tall_ref[columns(owner), 3 * width :]

    for i in far_first:
        g = lax.rem(group + i, groups)
        usend[i] = out_piece(g * 2 + 1 - half).astype(BF16)
        u_first(i).start()
        ukeep[i] = out_piece(g * 2 + half)
    for i in far_first[:-1]:
        t_first(i).wait_recv()
        tsum[i] = (tkeep[i] + tnear[i].astype(F32)).astype(BF16)
        t_second(i).start()
    for i in far_first[:-1]:
        u_first(i).wait_recv()
        usum[i] = (ukeep[i] + unear[i].astype(F32)).astype(BF16)
        u_second(i).start()
    for i in range(1, dp):
        count_copy(i).wait_recv()
    inverse = 1.0 / jnp.sum(tally[...], axis=0)[0:1]
    t_first(0).wait_recv()
    total = tkeep[0] + tnear[0].astype(F32)
    for i in far_first[:-1]:
        t_second(i).wait_recv()
        total += tfar[i].astype(F32)
    for j in range(3):
        part = total[j * width : (j + 1) * width].T if flat else total[:, j * width : (j + 1) * width]
        out_ref[j] = part * inverse
    u_first(0).wait_recv()
    total = ukeep[0] + unear[0].astype(F32)
    for i in far_first[:-1]:
        u_second(i).wait_recv()
        total += ufar[i].astype(F32)
    out2_ref[...] = (total if flat else total.T) * inverse[:, 0:1]

    for i in range(1, dp):
        frame_copy(i).wait_send()
        count_copy(i).wait_send()
        onward(i).wait_send()
    for c in across + beside + passed:
        c.wait_send()
    for a, b in others:
        for i in range(share):
            att_copy(a, b, i).wait_send()
            do_copy(a, b, i).wait_send()
    for c in range(pairs):
        o_first(c).wait_send()
        if c:
            o_second(c).wait_send()
    for i in range(groups):
        t_first(i).wait_send()
        u_first(i).wait_send()
        if i:
            t_second(i).wait_send()
            u_second(i).wait_send()


def finish_kernel(a_ref, b_ref, qkv_ref, o_ref):
    qkv_ref[...] = a_ref[...]
    o_ref[...] = b_ref[...]


def shards(
    dp, mp, noise_blocks, data_blocks, destination, utt_blocks, span_start, span_size, timestep,
    in_weight, norm_gain, qkv_weight, out_proj, final_gain, vel_weight,
):
    slots = noise_blocks.shape[0]
    mel = noise_blocks.shape[1] // BLOCK
    features = in_weight.shape[1]
    width = qkv_weight.shape[2]
    window = min(LONGEST, slots)
    heads = width // HEAD_DIM
    share, cols = slots // mp, features // dp
    pairs, groups = mp // 2, dp // 2
    flat = cols % LANES == 0
    big = (3 * width, cols) if flat else (cols, 3 * width)
    small = (width, cols) if flat else (cols, width)
    frames = jnp.concatenate([noise_blocks, data_blocks], axis=0).reshape(2, slots, BLOCK, mel)

    def array(shape, kind):
        return jax.ShapeDtypeStruct(shape, kind)

    def f32(*shape):
        return pltpu.VMEM(shape, F32)

    def bf16(*shape):
        return pltpu.VMEM(shape, BF16)

    def dma(*shape):
        return pltpu.SemaphoreType.DMA(shape)

    scratch = [
        bf16(2, slots, BLOCK, mel), bf16(2 * mel, features), bf16(2 * LANES, features),
        bf16(3, features, width), bf16(features, 3 * width), bf16(width, features), bf16(mel, features),
        dma(5), f32(8 if flat else features, 4 * width),
        bf16(dp, 2, BLOCK, LANES), bf16(dp, 2, BLOCK, LANES), f32(dp, 8, LANES),
        pltpu.SMEM((8, slots), I32), bf16(pairs, 2, width, features),
        f32(slots, BLOCK, features), bf16(slots, BLOCK, features), bf16(slots, BLOCK, 3 * width),
        f32(slots, heads * BLOCK, window * BLOCK), bf16(slots, window, heads * BLOCK, BLOCK),
        bf16(pairs, 2, share, BLOCK, width), bf16(pairs, 2, share, BLOCK, width),
        bf16(share, BLOCK, features), bf16(pairs, 2, share, BLOCK, width),
        bf16(pairs, 2, share, BLOCK, width), bf16(slots, BLOCK, width),
        bf16(slots, window, heads * BLOCK, BLOCK), bf16(slots, 3 * width, BLOCK),
        f32(pairs, width, features), bf16(pairs, width, features), bf16(pairs, width, features),
        bf16(pairs, width, features), bf16(pairs, width, features),
        f32(groups, *big), *[bf16(groups, *big)] * 4, f32(groups, *small), *[bf16(groups, *small)] * 4,
    ]
    scratch += [dma(dp)] * 6 + [dma(pairs, PIECES)] * 4 + [dma(pairs, 2, share)] * 4 + [dma(pairs)] * 4
    scratch += [dma(groups)] * 8
    sums, out_sum = pl.pallas_call(
        functools.partial(step_kernel, dp, mp),
        out_shape=(array((3, cols, width), F32), array((width, cols), F32)),
        in_specs=[SMEM] * 5 + [ANY, ANY, VMEM, ANY, ANY, VMEM, ANY],
        out_specs=(VMEM, VMEM),
        scratch_shapes=scratch,
        compiler_params=params(collective_id=0, has_side_effects=True),
        name="train_step",
    )(
        destination, utt_blocks, span_start, span_size, timestep, frames, in_weight, norm_gain,
        qkv_weight.transpose(1, 0, 2), out_proj, final_gain, vel_weight.T,
    )
    grad_qkv, grad_out = pl.pallas_call(
        finish_kernel,
        out_shape=(array((3, cols, width), F32), array((width, cols), F32)),
        in_specs=[VMEM, VMEM],
        out_specs=(VMEM, VMEM),
        compiler_params=params(),
        name="finish",
    )(sums, out_sum)
    return grad_qkv.transpose(1, 0, 2), grad_out


def solution(mesh):
    in_specs = (
        P("dp", None), P("dp", None), P(), P("dp", None), P("dp", None), P("dp", None),
        P("dp", None), P(), P(), P(None, None, "mp"), P("mp", None), P(), P(),
    )
    out_specs = (P("dp", None, "mp"), P("mp", "dp"))
    return jax.shard_map(
        functools.partial(shards, mesh.shape["dp"], mesh.shape["mp"]),
        mesh=mesh, in_specs=in_specs, out_specs=out_specs, check_vma=False,
    )
```

time: 93 us -> 59.1 us (0.64)
  Pallas kernels: 85.2 us -> 54.4 us
  local copies, waits for them, and re-layouts: 5.85 us -> 2.76 us
    pallas_call x5 -> x2, Pallas kernels: 85.2 us -> 54.4 us  [the longest x1 52.8 us: shards(): pl.pallas_call(functools.partial(step_kernel, dp, mp), out_shape=(array((...]
    unnamed x2 -> x0, local copies, waits for them, and re-layouts: 3.09 us -> none
where the time goes in v1:
time: 59.1 us; the launch traced here: 58.9 us
  Pallas kernels  54.4 us (92%)
  local copies, waits for them, and re-layouts  2.76 us (5%)
  other arithmetic  1.06 us (2%)
  between operations  0.64 us (1%)
    pallas_call x1, Pallas kernels, shards(): pl.pallas_call(functools.partial(step_kernel, dp, mp), out_shape=(array((...  52.8 us
    reshape x1, local copies, waits for them, and re-layouts, shards(): jnp.concatenate([noise_blocks, data_blocks], axis=0)  2.76 us
    pallas_call x1, Pallas kernels, shards(): pl.pallas_call(finish_kernel, out_shape=(array((3, cols, width), F32), ar...  1.64 us

profile of v1, /device:TPU:0, one launch (start us, length us, event | category | flops | bytes accessed | tf_op | source)
XLA Modules:
  0.0 58.9 jit_solution(192067777541208724)
XLA Ops:
  0.6 1.1 %pad_maximum_fusion = bf16[16,12800]{1,0:T(8,128)(2,1)S(1)} fusion(bf16[8,12800]{1,0:T(8,128)(2,1)} %param.14, bf16[8,12800]{1,0:T(8,128)(2,1)} %param.13), kind=kLoop, calls=%fused_computation | loop fusion | flops 819200 | bytes 819200 | tf_op jit(solution)/shard_map/concatenate | solution.py:549
  1.7 2.8 %reshape.7.x_hbm = bf16[2,8,128,100]{3,2,1,0:T(8,128)(2,1)} reshape(bf16[16,12800]{1,0:T(8,128)(2,1)S(1)} %pad_maximum_fusion) | data formatting | bytes 819200 | tf_op jit(solution)/shard_map/reshape | solution.py:549
  4.4 52.8 %train_step.1 = (f32[3,128,128]{2,1,0:T(8,128)}, f32[128,128]{1,0:T(8,128)}) custom-call(s32[64]{0:T(128)} %dest_ref.1, s32[1,4]{1,0:T(1,128)} %utt_ref.1, s32[1,4]{1,0:T(1,128)} %start_ref.1, s32[1,4]{1,0:T(1,128)} %size_ref.1, s32[1,4]{1,0:T(1,128)} %step_ref.1, bf16[2,8,128,100]{3,2,1,0:T(8,128)(2,1)} %reshape.7.x_hbm, bf16[200,1024]{1,0:T(8,128)(2,1)} %win_hbm.1, ...), custom_call_target="tpu_custom_call" | custom-call | tf_op jit(solution)/shard_map/train_step/pallas_call | solution.py:581
  57.3 1.6 %finish.1 = (f32[3,128,128]{2,1,0:T(8,128)}, f32[128,128]{1,0:T(8,128)}) custom-call(f32[3,128,128]{2,1,0:T(8,128)} %get-tuple-element.6.a_ref, f32[128,128]{1,0:T(8,128)} %get-tuple-element.7.b_ref), custom_call_target="tpu_custom_call" | custom-call | tf_op jit(solution)/shard_map/finish/pallas_call | solution.py:593

commit v2 on v1

--- a/solution.py
+++ b/solution.py
@@ -1,4 +1,5 @@
 import functools
+import math
 
 import jax
 import jax.numpy as jnp
@@ -56,25 +57,25 @@
 def step_kernel(
     dp, mp,
     dest_ref, utt_ref, start_ref, size_ref, step_ref,
-    x_hbm, win_hbm, gain_ref, wqkv_hbm, own_hbm, gain2_ref, vel_hbm,
+    noise_hbm, data_hbm, win_hbm, gain_ref, wqkv_hbm, own_hbm, gain2_ref, vel_hbm,
     out_ref, out2_ref,
-    x_ref, win_ref, wpad, wqkv, wcat, own_ref, vel_ref, lsem, tall_ref,
+    noise_ref, data_ref, flat_ref, spread, framed, target_ref, win_ref, wpad, wqkv, wcat, own_ref, vel_ref, lsem, tall_ref,
     stage, got, tally, tab, out_full,
     hid_ref, normed_ref, qkv_ref, p_ref, pb_ref, att_ref, all_ref, back_ref,
-    dosend, do_rel, do_ref, ds_ref, dt_ref,
+    dosend, do_rel, do_ref, ds_ref, dt_ref, dv_ref,
     okeep, osend, onear, osum, ofar,
-    tkeep, tsend, tnear, tsum, tfar,
-    ukeep, usend, unear, usum, ufar,
-    fsend, frecv, csend, crecv, hsend, hrecv,
-    wsend, wrecv, wfsend, wfrecv,
-    asend, arecv, dsend, drecv, o1s, o1r, o2s, o2r,
-    t1s, t1r, t2s, t2r, u1s, u1r, u2s, u2r,
+    *refs,
 ):
+    t_refs, v_refs, u_refs = (refs[n * 5 : n * 5 + 5] + refs[33 + n * 4 : 37 + n * 4] for n in range(3))
+    fsend, frecv, csend, crecv, hsend, hrecv = refs[15:21]
+    wsend, wrecv, wfsend, wfrecv, asend, arecv, dsend, drecv, o1s, o1r, o2s, o2r = refs[21:33]
     me, my = lax.axis_index("dp"), lax.axis_index("mp")
     slots = normed_ref.shape[0]
     features = normed_ref.shape[2]
     width = own_ref.shape[0]
-    mel = x_ref.shape[3]
+    mel = vel_ref.shape[0]
+    packed = BLOCK * mel // LANES
+    part_rows = got.shape[2]
     share = slots // mp
     pair, side = my // 2, lax.rem(my, 2)
     pairs = mp // 2
@@ -87,21 +88,32 @@
     wait = greet(dp, mp)
     loads = [
         pltpu.make_async_copy(a, b, lsem.at[n]) for n, (a, b) in enumerate((
-            (x_hbm, x_ref), (win_hbm, win_ref), (wqkv_hbm, wqkv), (own_hbm, own_ref), (vel_hbm, vel_ref),
+            (noise_hbm, noise_ref), (data_hbm, data_ref), (win_hbm, win_ref), (wqkv_hbm, wqkv),
+            (own_hbm, own_ref), (vel_hbm, vel_ref),
         ))
     ]
     for c in loads:
         c.start()
     owners = [dest_ref[me * slots + k] // slots for k in range(slots)]
-    stage[...] = jnp.zeros_like(stage)
+    flat_ref[pl.ds(2 * packed * slots, (2 * part_rows - 2 * packed) * slots)] = jnp.zeros(
+        ((2 * part_rows - 2 * packed) * slots, LANES), F32
+    )
     loads[0].wait()
+    loads[1].wait()
+    for part, ref in enumerate((noise_ref, data_ref)):
+        for r in range(packed):
+            flat_ref[pl.ds((part * packed + r) * slots, slots)] = (
+                ref[:, r * LANES : (r + 1) * LANES].astype(F32)
+            )
     for i in range(dp):
         to = lax.rem(me + i, dp)
         pick = jnp.int32(0)
         for k in range(slots):
             pick = jnp.where(owners[k] == to, k, pick)
         for part in range(2):
-            stage[i, part, :, 0:mel] = x_ref[part, pick]
+            stage[i, part] = flat_ref[
+                pl.ds(pick + part * part_rows * slots, part_rows, stride=slots)
+            ].astype(BF16)
     count = jnp.int32(0)
     for u in range(utt_ref.shape[1]):
         low = start_ref[0, u]
@@ -109,18 +121,17 @@
         count += (high - low) * utt_ref[0, u] * (BLOCK // 64)
     tally[0] = jnp.full(tally.shape[1:], count, I32).astype(F32)
     got[0] = stage[0]
-    lines = pl.ds(pl.multiple_of(side * (BLOCK // 2), BLOCK // 2), BLOCK // 2)
     wait()
 
     def frame_copy(i):
         return remote(
-            stage.at[i, :, lines], got.at[i, :, lines], fsend.at[i], frecv.at[i],
+            stage.at[i, side], got.at[i, side], fsend.at[i], frecv.at[i],
             (lax.rem(me + i, dp), my),
         )
 
     def onward(i):
         return remote(
-            got.at[i, :, lines], got.at[i, :, lines], hsend.at[i], hrecv.at[i], (me, mate)
+            got.at[i, side], got.at[i, side], hsend.at[i], hrecv.at[i], (me, mate)
         )
 
     def count_copy(i):
@@ -131,7 +142,7 @@
         frame_copy(i).start()
     for i in order:
         count_copy(i).start()
-    loads[3].wait()
+    loads[4].wait()
     piece = width // PIECES
 
     def full_at(a, b, p):
@@ -188,11 +199,11 @@
         tab[HIGH, s] = high
         tab[STEP, s] = step
 
-    loads[1].wait()
+    loads[2].wait()
     wpad[...] = jnp.zeros_like(wpad)
     wpad[0:mel] = win_ref[0:mel]
     wpad[LANES : LANES + mel] = win_ref[mel : 2 * mel]
-    loads[2].wait()
+    loads[3].wait()
     for j in range(3):
         wcat[:, j * width : (j + 1) * width] = wqkv[j]
     gain = gain_ref[...].astype(F32).reshape(1, -1)
@@ -201,16 +212,42 @@
         frame = (tab[POS, s] - tab[FIRST, s]) * BLOCK + lax.broadcasted_iota(I32, (BLOCK, 1), 0)
         return ((frame >= tab[LOW, s]) & (frame < tab[HIGH, s])).astype(F32)
 
-    def inputs_of(s):
+    cycle = math.lcm(mel, LANES) // mel
+    turns, pitch = BLOCK // cycle, cycle + 8
+    stride = cycle * mel // LANES
+    lanes = lax.broadcasted_iota(I32, (1, LANES), 1)
+
+    def frames_of(s, n):
         src = s if aligned else tab[SOURCE, s]
-        noise, data = got[src, 0].astype(F32), got[src, 1].astype(F32)
+        for part in range(2):
+            spread[n, part * part_rows : (part + 1) * part_rows] = got[src, part].astype(F32)
+        for f in range(cycle):
+            row, shift = f * mel // LANES, f * mel % LANES
+            a = spread[n, pl.ds(row, 2 * turns, stride=stride)]
+            if shift + mel > LANES:
+                b = spread[n, pl.ds(row + 1, 2 * turns, stride=stride)]
+                a = jnp.where(lanes >= shift, a, b)
+            if shift:
+                a = pltpu.roll(a, LANES - shift, axis=1)
+            framed[n, pl.ds(f, 2 * turns, stride=pitch)] = a
+        return [
+            jnp.concatenate(
+                [framed[n, (part * turns + t) * pitch : (part * turns + t) * pitch + cycle] for t in range(turns)],
+                axis=0,
+            )
+            for part in range(2)
+        ]
+
+    def inputs_of(s, n):
+        noise, data = frames_of(s, n)
+        target_ref[s] = data - noise
         level = jnp.full((1, 1), tab[STEP, s], I32).astype(F32) / 64.0
         noisy = (1.0 - level) * noise + level * data
         cond = data * (1.0 - masked_of(s))
         return jnp.concatenate([noisy, cond], axis=1).astype(BF16)
 
     def encode(pieces):
-        hidden = dot(jnp.concatenate([inputs_of(s) for s in pieces], axis=0), wpad[...])
+        hidden = dot(jnp.concatenate([inputs_of(s, n) for n, s in enumerate(pieces)], axis=0), wpad[...])
         scale = lax.rsqrt(jnp.mean(hidden * hidden, axis=1, keepdims=True) + 1e-06)
         normed = (hidden * scale * gain).astype(BF16)
         qkv = dot(normed, wcat[...]).astype(BF16)
@@ -322,7 +359,7 @@
         c.wait_recv()
     for f in passed:
         f.wait_recv()
-    loads[4].wait()
+    loads[5].wait()
     gain2 = gain2_ref[...].astype(F32).reshape(1, -1)
     for a, b in others:
         for i in range(share):
@@ -346,9 +383,7 @@
         rscale = lax.rsqrt(jnp.mean(wide * wide, axis=1, keepdims=True) + 1e-06)
         normalized = wide * rscale
         velocity = dot((normalized * gain2).astype(BF16), vel_ref[...], NT)
-        src = s if aligned else tab[SOURCE, s]
-        target = (got[src, 1].astype(F32) - got[src, 0].astype(F32))[:, 0:mel]
-        error = (2.0 * masked_of(s) * (velocity - target)).astype(BF16)
+        error = (2.0 * masked_of(s) * (velocity - target_ref[s, :, 0:mel])).astype(BF16)
         scaled = dot(error, vel_ref[...]) * gain2
         back = (
             rscale * (scaled - normalized * jnp.mean(scaled * normalized, axis=1, keepdims=True))
@@ -381,16 +416,98 @@
         okeep[c] = out_term(c, 0)
 
     for u, (a, b) in enumerate(spots[::-1]):
-        if u == 2:
-            for c in range(1, pairs):
-                o_first(c).wait_recv()
-                osum[c] = (okeep[c] + onear[c].astype(F32)).astype(BF16)
-                o_second(c).start()
         for i in range(share):
-            s = first_slot(a, b) + i
             if u:
                 do_copy((pairs - a) % pairs, b, i).wait_recv()
-                do_ref[s] = do_rel[a, b, i]
+                do_ref[first_slot(a, b) + i] = do_rel[a, b, i]
+
+    def pick(ref, s):
+        begin, at, valid = window_of(s)
+        own = jnp.clip(tab[POS, s] - begin, 0, window - 1)
+        return at, jnp.concatenate(
+            [jnp.where(valid[i], ref[at[i], own], BF16(0)) for i in range(window)], axis=0
+        )
+
+    def values_step(s, _):
+        at, probs = pick(pb_ref, s)
+        couts = jnp.concatenate([split(do_ref[i]) for i in at], axis=0)
+        dv_ref[s] = dot(couts, probs, TN).astype(BF16)
+        return 0
+
+    lax.fori_loop(0, slots, values_step, 0, unroll=2)
+
+    for c in range(1, pairs):
+        o_first(c).wait_recv()
+        osum[c] = (okeep[c] + onear[c].astype(F32)).astype(BF16)
+        o_second(c).start()
+
+    cols = features // dp
+    flat = cols % LANES == 0
+    far_first = sorted(range(1, groups), key=lambda i: -min(i, groups - i)) + [0]
+
+    def columns(owner):
+        return pl.ds(pl.multiple_of(owner * cols, cols), cols)
+
+    class Reduction:
+        def __init__(self, refs, term):
+            self.keep, self.out, self.near, self.sum, self.far, *self.sems = refs
+            self.term = term
+
+        def first(self, i):
+            s1, r1, _, _ = self.sems
+            return remote(self.out.at[i], self.near.at[i], s1.at[i], r1.at[i], (partner, my))
+
+        def second(self, i):
+            _, _, s2, r2 = self.sems
+            g = lax.rem(group + i, groups)
+            return remote(self.sum.at[i], self.far.at[i], s2.at[i], r2.at[i], (g * 2 + half, my))
+
+        def begin(self):
+            for i in far_first:
+                g = lax.rem(group + i, groups)
+                self.out[i] = self.term(g * 2 + 1 - half).astype(BF16)
+                self.first(i).start()
+                self.keep[i] = self.term(g * 2 + half)
+
+        def middle(self):
+            for i in far_first[:-1]:
+                self.first(i).wait_recv()
+                self.sum[i] = (self.keep[i] + self.near[i].astype(F32)).astype(BF16)
+                self.second(i).start()
+
+        def end(self):
+            self.first(0).wait_recv()
+            total = self.keep[0] + self.near[0].astype(F32)
+            for i in far_first[:-1]:
+                self.second(i).wait_recv()
+                total += self.far[i].astype(F32)
+            return total
+
+        def drain(self):
+            for i in range(groups):
+                self.first(i).wait_send()
+                if i:
+                    self.second(i).wait_send()
+
+    def product(ref, at):
+        parts = jnp.concatenate([ref[s] for s in range(slots)], axis=1)
+        rows = parts.shape[0]
+        if flat:
+            return lambda owner: dot(
+                parts,
+                jnp.concatenate([normed_ref[s, :, columns(owner)] for s in range(slots)], axis=0),
+            )
+        normed = jnp.concatenate([normed_ref[s] for s in range(slots)], axis=0)
+        for n in range(0, rows, width):
+            tall_ref[:, at + n : at + n + width] = dot(parts[n : n + width], normed).T
+        return lambda owner: tall_ref[columns(owner), at : at + rows]
+
+    values = Reduction(v_refs, product(dv_ref, 2 * width))
+    values.begin()
+
+    for u, (a, b) in enumerate(spots[::-1]):
+        if u == mp // 2:
+            values.middle()
         for i in range(share):
             s = first_slot(a, b) + i
             _, at, _ = window_of(s)
@@ -403,63 +520,15 @@
             dt_ref[s, 0:width] = dq.T.astype(BF16)
 
     def keys_step(s, _):
-        begin, at, valid = window_of(s)
-        own = jnp.clip(tab[POS, s] - begin, 0, window - 1)
-
-        def pick(ref):
-            return jnp.concatenate(
-                [jnp.where(valid[i], ref[at[i], own], BF16(0)) for i in range(window)], axis=0
-            )
-
+        at, ds = pick(ds_ref, s)
         queries = jnp.concatenate([query_of(i) for i in at], axis=0)
-        couts = jnp.concatenate([split(do_ref[i]) for i in at], axis=0)
-        dt_ref[s, width : 2 * width] = dot(queries, pick(ds_ref), TN).astype(BF16)
-        dt_ref[s, 2 * width :] = dot(couts, pick(pb_ref), TN).astype(BF16)
+        dt_ref[s, width : 2 * width] = dot(queries, ds, TN).astype(BF16)
         return 0
 
-    lax.fori_loop(0, slots, keys_step, 0)
-
-    d_all = jnp.concatenate([dt_ref[s] for s in range(slots)], axis=1)
-
-    def t_first(i):
-        return remote(tsend.at[i], tnear.at[i], t1s.at[i], t1r.at[i], (partner, my))
-
-    def t_second(i):
-        g = lax.rem(group + i, groups)
-        return remote(tsum.at[i], tfar.at[i], t2s.at[i], t2r.at[i], (g * 2 + half, my))
-
-    def u_first(i):
-        return remote(usend.at[i], unear.at[i], u1s.at[i], u1r.at[i], (partner, my))
-
-    def u_second(i):
-        g = lax.rem(group + i, groups)
-        return remote(usum.at[i], ufar.at[i], u2s.at[i], u2r.at[i], (g * 2 + half, my))
-
-    cols = features // dp
-    flat = cols % LANES == 0
-
-    def columns(owner):
-        return pl.ds(pl.multiple_of(owner * cols, cols), cols)
-
-    if flat:
-        def term(owner):
-            normed = jnp.concatenate([normed_ref[s, :, columns(owner)] for s in range(slots)], axis=0)
-            return dot(d_all, normed)
-    else:
-        normed_all = jnp.concatenate([normed_ref[s] for s in range(slots)], axis=0)
-        for j in range(3):
-            rows = d_all[j * width : (j + 1) * width]
-            tall_ref[:, j * width : (j + 1) * width] = dot(rows, normed_all).T
-
-        def term(owner):
-            return tall_ref[columns(owner), 0 : 3 * width]
-
-    far_first = sorted(range(1, groups), key=lambda i: -min(i, groups - i)) + [0]
-    for i in far_first:
-        g = lax.rem(group + i, groups)
-        tsend[i] = term(g * 2 + 1 - half).astype(BF16)
-        t_first(i).start()
-        tkeep[i] = term(g * 2 + half)
+    lax.fori_loop(0, slots, keys_step, 0, unroll=2)
+
+    others_of = Reduction(t_refs, product(dt_ref, 0))
+    others_of.begin()
     o_first(0).wait_recv()
     total = okeep[0] + onear[0].astype(F32)
     for c in range(1, pairs):
@@ -467,41 +536,23 @@
         total += ofar[c].astype(F32)
     if flat:
         okeep[0] = total
+        outs = Reduction(u_refs, lambda owner: okeep[0, :, columns(owner)])
     else:
         tall_ref[:, 3 * width :] = total.T
-
-    def out_piece(owner):
-        return okeep[0, :, columns(owner)] if flat else tall_ref[columns(owner), 3 * width :]
-
-    for i in far_first:
-        g = lax.rem(group + i, groups)
-        usend[i] = out_piece(g * 2 + 1 - half).astype(BF16)
-        u_first(i).start()
-        ukeep[i] = out_piece(g * 2 + half)
-    for i in far_first[:-1]:
-        t_first(i).wait_recv()
-        tsum[i] = (tkeep[i] + tnear[i].astype(F32)).astype(BF16)
-        t_second(i).start()
-    for i in far_first[:-1]:
-        u_first(i).wait_recv()
-        usum[i] = (ukeep[i] + unear[i].astype(F32)).astype(BF16)
-        u_second(i).start()
+        outs = Reduction(u_refs, lambda owner: tall_ref[columns(owner), 3 * width :])
+    outs.begin()
+    others_of.middle()
+    outs.middle()
     for i in range(1, dp):
         count_copy(i).wait_recv()
     inverse = 1.0 / jnp.sum(tally[...], axis=0)[0:1]
-    t_first(0).wait_recv()
-    total = tkeep[0] + tnear[0].astype(F32)
-    for i in far_first[:-1]:
-        t_second(i).wait_recv()
-        total += tfar[i].astype(F32)
-    for j in range(3):
+    total = values.end()
+    out_ref[2] = (total.T if flat else total) * inverse
+    total = others_of.end()
+    for j in range(2):
         part = total[j * width : (j + 1) * width].T if flat else total[:, j * width : (j + 1) * width]
         out_ref[j] = part * inverse
-    u_first(0).wait_recv()
-    total = ukeep[0] + unear[0].astype(F32)
-    for i in far_first[:-1]:
-        u_second(i).wait_recv()
-        total += ufar[i].astype(F32)
+    total = outs.end()
     out2_ref[...] = (total if flat else total.T) * inverse[:, 0:1]
 
     for i in range(1, dp):
@@ -518,12 +569,8 @@
         o_first(c).wait_send()
         if c:
             o_second(c).wait_send()
-    for i in range(groups):
-        t_first(i).wait_send()
-        u_first(i).wait_send()
-        if i:
-            t_second(i).wait_send()
-            u_second(i).wait_send()
+    for reduction in (values, others_of, outs):
+        reduction.drain()
 
 
 def finish_kernel(a_ref, b_ref, qkv_ref, o_ref):
@@ -544,9 +591,10 @@
     share, cols = slots // mp, features // dp
     pairs, groups = mp // 2, dp // 2
     flat = cols % LANES == 0
-    big = (3 * width, cols) if flat else (cols, 3 * width)
-    small = (width, cols) if flat else (cols, width)
-    frames = jnp.concatenate([noise_blocks, data_blocks], axis=0).reshape(2, slots, BLOCK, mel)
+    shapes = [(n * width, cols) if flat else (cols, n * width) for n in (2, 1, 1)]
+    packed = BLOCK * mel // LANES
+    part_rows = (packed + 7) // 8 * 8
+    cycle = math.lcm(mel, LANES) // mel
 
     def array(shape, kind):
         return jax.ShapeDtypeStruct(shape, kind)
@@ -561,33 +609,37 @@
         return pltpu.SemaphoreType.DMA(shape)
 
     scratch = [
-        bf16(2, slots, BLOCK, mel), bf16(2 * mel, features), bf16(2 * LANES, features),
+        bf16(slots, BLOCK * mel), bf16(slots, BLOCK * mel), f32(2 * part_rows * slots, LANES),
+        f32(2, 2 * part_rows, LANES), f32(2, 2 * (BLOCK // cycle) * (cycle + 8), LANES),
+        f32(slots, BLOCK, LANES), bf16(2 * mel, features), bf16(2 * LANES, features),
         bf16(3, features, width), bf16(features, 3 * width), bf16(width, features), bf16(mel, features),
-        dma(5), f32(8 if flat else features, 4 * width),
-        bf16(dp, 2, BLOCK, LANES), bf16(dp, 2, BLOCK, LANES), f32(dp, 8, LANES),
+        dma(6), f32(8 if flat else features, 4 * width),
+        bf16(dp, 2, part_rows, LANES), bf16(dp, 2, part_rows, LANES), f32(dp, 8, LANES),
         pltpu.SMEM((8, slots), I32), bf16(pairs, 2, width, features),
         f32(slots, BLOCK, features), bf16(slots, BLOCK, features), bf16(slots, BLOCK, 3 * width),
         f32(slots, heads * BLOCK, window * BLOCK), bf16(slots, window, heads * BLOCK, BLOCK),
         bf16(pairs, 2, share, BLOCK, width), bf16(pairs, 2, share, BLOCK, width),
         bf16(share, BLOCK, features), bf16(pairs, 2, share, BLOCK, width),
         bf16(pairs, 2, share, BLOCK, width), bf16(slots, BLOCK, width),
-        bf16(slots, window, heads * BLOCK, BLOCK), bf16(slots, 3 * width, BLOCK),
+        bf16(slots, window, heads * BLOCK, BLOCK), bf16(slots, 2 * width, BLOCK), bf16(slots, width, BLOCK),
         f32(pairs, width, features), bf16(pairs, width, features), bf16(pairs, width, features),
         bf16(pairs, width, features), bf16(pairs, width, features),
-        f32(groups, *big), *[bf16(groups, *big)] * 4, f32(groups, *small), *[bf16(groups, *small)] * 4,
     ]
+    for shape in shapes:
+        scratch += [f32(groups, *shape)] + [bf16(groups, *shape)] * 4
     scratch += [dma(dp)] * 6 + [dma(pairs, PIECES)] * 4 + [dma(pairs, 2, share)] * 4 + [dma(pairs)] * 4
-    scratch += [dma(groups)] * 8
+    scratch += [dma(groups)] * 12
     sums, out_sum = pl.pallas_call(
         functools.partial(step_kernel, dp, mp),
-        out_shape=(array((3, cols, width), F32), array((width, cols), F32)),
-        in_specs=[SMEM] * 5 + [ANY, ANY, VMEM, ANY, ANY, VMEM, ANY],
+        out_shape=(f32(3, cols, width), f32(width, cols)),
+        in_specs=[SMEM] * 5 + [ANY, ANY, ANY, VMEM, ANY, ANY, VMEM, ANY],
         out_specs=(VMEM, VMEM),
         scratch_shapes=scratch,
         compiler_params=params(collective_id=0, has_side_effects=True),
         name="train_step",
     )(
-        destination, utt_blocks, span_start, span_size, timestep, frames, in_weight, norm_gain,
+        destination, utt_blocks, span_start, span_size, timestep, noise_blocks, data_blocks,
+        in_weight, norm_gain,
         qkv_weight.transpose(1, 0, 2), out_proj, final_gain, vel_weight.T,
     )
     grad_qkv, grad_out = pl.pallas_call(
@@ -597,7 +649,10 @@
         out_specs=(VMEM, VMEM),
         compiler_params=params(),
         name="finish",
-    )(sums, out_sum)
+    )(
+        pltpu.with_memory_space_constraint(sums, pltpu.VMEM),
+        pltpu.with_memory_space_constraint(out_sum, pltpu.VMEM),
+    )
     return grad_qkv.transpose(1, 0, 2), grad_out
 
 

time: 59.1 us -> 53 us (0.90)
  local copies, waits for them, and re-layouts: 2.76 us -> 0 us
  Pallas kernels: 54.4 us -> 52.2 us
  other arithmetic: 1.06 us -> 0 us
    reshape x1 -> x0, local copies, waits for them, and re-layouts: 2.76 us -> none  [shards(): jnp.concatenate([noise_blocks, data_blocks], axis=0)]
    pallas_call x1, Pallas kernels: 52.8 us -> 51.5 us  [shards(): pl.pallas_call(functools.partial(step_kernel, dp, mp), out_shape=(f32(3,...]
    concatenate x1 -> x0, other arithmetic: 1.06 us -> none  [shards(): jnp.concatenate([noise_blocks, data_blocks], axis=0)]
    pallas_call x1, Pallas kernels: 1.64 us -> 0.71 us  [shards(): pl.pallas_call(finish_kernel, out_shape=(array((3, cols, width), F32), ar...]
where the time goes in v2:
time: 53 us; the launch traced here: 52.8 us
  Pallas kernels  52.2 us (98%)
  between operations  0.64 us (1%)
    pallas_call x1, Pallas kernels, shards(): pl.pallas_call(functools.partial(step_kernel, dp, mp), out_shape=(f32(3,...  51.5 us

profile of v2, /device:TPU:0, one launch (start us, length us, event | category | flops | bytes accessed | tf_op | source)
XLA Modules:
  0.0 52.8 jit_solution(134971124483082163)
XLA Ops:
  0.6 51.5 %train_step.1 = (f32[3,128,128]{2,1,0:T(8,128)S(1)}, f32[128,128]{1,0:T(8,128)S(1)}) custom-call(s32[64]{0:T(128)} %dest_ref.1, s32[1,4]{1,0:T(1,128)} %utt_ref.1, s32[1,4]{1,0:T(1,128)} %start_ref.1, s32[1,4]{1,0:T(1,128)} %size_ref.1, s32[1,4]{1,0:T(1,128)} %step_ref.1, bf16[8,12800]{1,0:T(8,128)(2,1)} %noise_hbm.1, bf16[8,12800]{1,0:T(8,128)(2,1)} %data_hbm.1, ...), custom_call_target="tpu_custom_call" | custom-call | tf_op jit(solution)/shard_map/train_step/pallas_call | solution.py:632
  52.1 0.7 %finish.1 = (f32[3,128,128]{2,1,0:T(8,128)}, f32[128,128]{1,0:T(8,128)}) custom-call(f32[3,128,128]{2,1,0:T(8,128)S(1)} %get-tuple-element.6.a_ref, f32[128,128]{1,0:T(8,128)S(1)} %get-tuple-element.7.b_ref), custom_call_target="tpu_custom_call" | custom-call | tf_op jit(solution)/shard_map/finish/pallas_call | solution.py:645

commit v3 on v2

--- a/solution.py
+++ b/solution.py
@@ -66,9 +66,9 @@
     okeep, osend, onear, osum, ofar,
     *refs,
 ):
-    t_refs, v_refs, u_refs = (refs[n * 5 : n * 5 + 5] + refs[33 + n * 4 : 37 + n * 4] for n in range(3))
-    fsend, frecv, csend, crecv, hsend, hrecv = refs[15:21]
-    wsend, wrecv, wfsend, wfrecv, asend, arecv, dsend, drecv, o1s, o1r, o2s, o2r = refs[21:33]
+    t_refs, v_refs, u_refs = (refs[n * 3 : n * 3 + 3] + refs[27 + n * 2 : 29 + n * 2] for n in range(3))
+    fsend, frecv, csend, crecv, hsend, hrecv = refs[9:15]
+    wsend, wrecv, wfsend, wfrecv, asend, arecv, dsend, drecv, o1s, o1r, o2s, o2r = refs[15:27]
     me, my = lax.axis_index("dp"), lax.axis_index("mp")
     slots = normed_ref.shape[0]
     features = normed_ref.shape[2]
@@ -80,9 +80,6 @@
     pair, side = my // 2, lax.rem(my, 2)
     pairs = mp // 2
     mate = pair * 2 + 1 - side
-    group, half = me // 2, lax.rem(me, 2)
-    groups = dp // 2
-    partner = group * 2 + 1 - half
     aligned = dp == slots
 
     wait = greet(dp, mp)
@@ -352,6 +349,7 @@
     for a, b in others:
         for i in range(share):
             att_ref[a, b, i] = attend(first_slot(pairs - a, b) + i)
+        for i in range(share):
             att_copy(a, b, i).start()
     for i in range(share):
         all_ref[0, 0, i] = attend(my * share + i)
@@ -361,9 +359,6 @@
         f.wait_recv()
     loads[5].wait()
     gain2 = gain2_ref[...].astype(F32).reshape(1, -1)
-    for a, b in others:
-        for i in range(share):
-            att_copy(a, b, i).wait_recv()
     full = jnp.concatenate([out_full[a, b] for a, b in spots], axis=0)
 
     def do_copy(a, b, i):
@@ -373,32 +368,38 @@
             device_at(a, b),
         )
 
-    for i in range(share):
-        s = my * share + i
-        mixed = None
-        for a, b in spots:
-            part = dot(all_ref[a, b, i], out_full[a, b]).astype(BF16).astype(F32)
-            mixed = part if mixed is None else mixed + part
-        wide = (hid_ref[s] + mixed).astype(BF16).astype(F32)
-        rscale = lax.rsqrt(jnp.mean(wide * wide, axis=1, keepdims=True) + 1e-06)
-        normalized = wide * rscale
-        velocity = dot((normalized * gain2).astype(BF16), vel_ref[...], NT)
-        error = (2.0 * masked_of(s) * (velocity - target_ref[s, :, 0:mel])).astype(BF16)
-        scaled = dot(error, vel_ref[...]) * gain2
-        back = (
-            rscale * (scaled - normalized * jnp.mean(scaled * normalized, axis=1, keepdims=True))
-        ).astype(BF16)
-        back_ref[i] = back
-        do = dot(back, full, NT).astype(BF16)
-        for n, (a, b) in enumerate(spots):
-            piece_do = do[:, n * width : (n + 1) * width]
+    def own_rows(ref):
+        return jnp.concatenate([ref[my * share + i] for i in range(share)], axis=0)
+
+    mixed = None
+    for a, b in spots[::-1]:
+        if (a, b) != (0, 0):
+            for i in range(share):
+                att_copy(a, b, i).wait_recv()
+        rows = jnp.concatenate([all_ref[a, b, i] for i in range(share)], axis=0)
+        part = dot(rows, out_full[a, b]).astype(BF16).astype(F32)
+        mixed = part if mixed is None else mixed + part
+    masked = jnp.concatenate([masked_of(my * share + i) for i in range(share)], axis=0)
+    wide = (own_rows(hid_ref) + mixed).astype(BF16).astype(F32)
+    rscale = lax.rsqrt(jnp.mean(wide * wide, axis=1, keepdims=True) + 1e-06)
+    normalized = wide * rscale
+    velocity = dot((normalized * gain2).astype(BF16), vel_ref[...], NT)
+    error = (2.0 * masked * (velocity - own_rows(target_ref)[:, 0:mel])).astype(BF16)
+    scaled = dot(error, vel_ref[...]) * gain2
+    back = (
+        rscale * (scaled - normalized * jnp.mean(scaled * normalized, axis=1, keepdims=True))
+    ).astype(BF16)
+    do = dot(back, full, NT).astype(BF16)
+    for n, (a, b) in enumerate(spots):
+        for i in range(share):
+            piece_do = do[i * BLOCK : (i + 1) * BLOCK, n * width : (n + 1) * width]
             if (a, b) == (0, 0):
-                do_ref[s] = piece_do
+                do_ref[my * share + i] = piece_do
             else:
                 dosend[a, b, i] = piece_do
-                do_copy(a, b, i).start()
-
-    back = jnp.concatenate([back_ref[i] for i in range(share)], axis=0)
+    for a, b in others:
+        for i in range(share):
+            do_copy(a, b, i).start()
 
     def out_term(a, b):
         return dot(jnp.concatenate([all_ref[a, b, i] for i in range(share)], axis=0), back, TN)
@@ -415,11 +416,26 @@
     for c in range(pairs):
         okeep[c] = out_term(c, 0)
 
-    for u, (a, b) in enumerate(spots[::-1]):
+    def pull(s):
+        _, at, _ = window_of(s)
+        probs = p_ref[s]
+        dprobs = dot(split(do_ref[s]), window_cols(at, 2), NT).astype(BF16).astype(F32)
+        ds = (probs * (dprobs - jnp.sum(dprobs * probs, axis=1, keepdims=True))).astype(BF16)
+        for n in range(window):
+            ds_ref[s, n] = ds[:, n * BLOCK : (n + 1) * BLOCK]
+        dq = merge(dot(ds, window_cols(at, 1))) * (HEAD_DIM**-0.5)
+        dt_ref[s, 0:width] = dq.T.astype(BF16)
+
+    for i in range(share):
+        pull(my * share + i)
+    for c in range(1, pairs):
+        o_first(c).wait_recv()
+        osum[c] = (okeep[c] + onear[c].astype(F32)).astype(BF16)
+        o_second(c).start()
+    for a, b in others[::-1]:
         for i in range(share):
-            if u:
-                do_copy((pairs - a) % pairs, b, i).wait_recv()
-                do_ref[first_slot(a, b) + i] = do_rel[a, b, i]
+            do_copy((pairs - a) % pairs, b, i).wait_recv()
+            do_ref[first_slot(a, b) + i] = do_rel[a, b, i]
 
     def pick(ref, s):
         begin, at, valid = window_of(s)
@@ -436,58 +452,95 @@
 
     lax.fori_loop(0, slots, values_step, 0, unroll=2)
 
-    for c in range(1, pairs):
-        o_first(c).wait_recv()
-        osum[c] = (okeep[c] + onear[c].astype(F32)).astype(BF16)
-        o_second(c).start()
-
     cols = features // dp
     flat = cols % LANES == 0
-    far_first = sorted(range(1, groups), key=lambda i: -min(i, groups - i)) + [0]
+
+    def flipped(r):
+        to = me
+        for bit in range(r.bit_length()):
+            if r >> bit & 1:
+                to = to + (1 - 2 * lax.rem(me // 2**bit, 2)) * 2**bit
+        return to
 
     def columns(owner):
         return pl.ds(pl.multiple_of(owner * cols, cols), cols)
 
     class Reduction:
-        def __init__(self, refs, term):
-            self.keep, self.out, self.near, self.sum, self.far, *self.sems = refs
-            self.term = term
-
-        def first(self, i):
-            s1, r1, _, _ = self.sems
-            return remote(self.out.at[i], self.near.at[i], s1.at[i], r1.at[i], (partner, my))
-
-        def second(self, i):
-            _, _, s2, r2 = self.sems
-            g = lax.rem(group + i, groups)
-            return remote(self.sum.at[i], self.far.at[i], s2.at[i], r2.at[i], (g * 2 + half, my))
+        def __init__(self, refs, bits, term):
+            self.keep, self.out, self.near, self.sent, self.came = refs
+            self.bits, self.term = bits, term
+
+        def pieces(self, n):
+            later = [0]
+            for bit in self.bits[n + 1 :][::-1]:
+                later = [r | bit for r in later] + later
+            return later
+
+        def copy(self, n, r):
+            r = r | self.bits[n]
+            return remote(
+                self.out.at[r], self.near.at[r], self.sent.at[r], self.came.at[r],
+                (flipped(self.bits[n]), my),
+            )
+
+        def total(self, n, r):
+            value = self.keep[r]
+            for p in range(n):
+                self.copy(p, r).wait_recv()
+                value += self.near[r | self.bits[p]].astype(F32)
+            return value
 
         def begin(self):
-            for i in far_first:
-                g = lax.rem(group + i, groups)
-                self.out[i] = self.term(g * 2 + 1 - half).astype(BF16)
-                self.first(i).start()
-                self.keep[i] = self.term(g * 2 + half)
-
-        def middle(self):
-            for i in far_first[:-1]:
-                self.first(i).wait_recv()
-                self.sum[i] = (self.keep[i] + self.near[i].astype(F32)).astype(BF16)
-                self.second(i).start()
+            for r in self.pieces(0):
+                self.out[r | self.bits[0]] = self.term(flipped(r | self.bits[0])).astype(BF16)
+                self.copy(0, r).start()
+
+        def hold(self):
+            for r in self.pieces(0):
+                self.keep[r] = self.term(flipped(r))
+
+        def stage(self, n):
+            for r in self.pieces(n):
+                r = r | self.bits[n]
+                self.out[r] = self.total(n, r).astype(BF16)
+                self.copy(n, r ^ self.bits[n]).start()
 
         def end(self):
-            self.first(0).wait_recv()
-            total = self.keep[0] + self.near[0].astype(F32)
-            for i in far_first[:-1]:
-                self.second(i).wait_recv()
-                total += self.far[i].astype(F32)
-            return total
+            return self.total(len(self.bits), 0)
 
         def drain(self):
-            for i in range(groups):
-                self.first(i).wait_send()
-                if i:
-                    self.second(i).wait_send()
+            for n in range(len(self.bits)):
+                for r in self.pieces(n):
+                    self.copy(n, r).wait_send()
+
+    class Direct(Reduction):
+        def second(self, r):
+            return remote(
+                self.out.at[r], self.near.at[r], self.sent.at[r], self.came.at[r], (flipped(r), my)
+            )
+
+        def stage(self, n):
+            if n == 1:
+                for r in self.far:
+                    self.out[r] = self.total(1, r).astype(BF16)
+                    self.second(r).start()
+
+        @property
+        def far(self):
+            return [r for r in self.pieces(0) if r]
+
+        def end(self):
+            value = self.total(1, 0)
+            for r in self.far:
+                self.second(r).wait_recv()
+                value += self.near[r].astype(F32)
+            return value
+
+        def drain(self):
+            for r in self.pieces(0):
+                self.copy(0, r).wait_send()
+            for r in self.far:
+                self.second(r).wait_send()
 
     def product(ref, at):
         parts = jnp.concatenate([ref[s] for s in range(slots)], axis=1)
@@ -502,22 +555,17 @@
             tall_ref[:, at + n : at + n + width] = dot(parts[n : n + width], normed).T
         return lambda owner: tall_ref[columns(owner), at : at + rows]
 
-    values = Reduction(v_refs, product(dv_ref, 2 * width))
+    bits = [2**n for n in range(dp.bit_length() - 1)]
+    stages = range(2, len(bits))
+    values = Direct(v_refs, bits, product(dv_ref, 2 * width))
     values.begin()
-
-    for u, (a, b) in enumerate(spots[::-1]):
+    values.hold()
+
+    for u, (a, b) in enumerate(others[::-1]):
         if u == mp // 2:
-            values.middle()
+            values.stage(1)
         for i in range(share):
-            s = first_slot(a, b) + i
-            _, at, _ = window_of(s)
-            probs = p_ref[s]
-            dprobs = dot(split(do_ref[s]), window_cols(at, 2), NT).astype(BF16).astype(F32)
-            ds = (probs * (dprobs - jnp.sum(dprobs * probs, axis=1, keepdims=True))).astype(BF16)
-            for n in range(window):
-                ds_ref[s, n] = ds[:, n * BLOCK : (n + 1) * BLOCK]
-            dq = merge(dot(ds, window_cols(at, 1))) * (HEAD_DIM**-0.5)
-            dt_ref[s, 0:width] = dq.T.astype(BF16)
+            pull(first_slot(a, b) + i)
 
     def keys_step(s, _):
         at, ds = pick(ds_ref, s)
@@ -527,7 +575,7 @@
 
     lax.fori_loop(0, slots, keys_step, 0, unroll=2)
 
-    others_of = Reduction(t_refs, product(dt_ref, 0))
+    others_of = Direct(t_refs, bits, product(dt_ref, 0))
     others_of.begin()
     o_first(0).wait_recv()
     total = okeep[0] + onear[0].astype(F32)
@@ -536,13 +584,16 @@
         total += ofar[c].astype(F32)
     if flat:
         okeep[0] = total
-        outs = Reduction(u_refs, lambda owner: okeep[0, :, columns(owner)])
+        outs = Reduction(u_refs, bits[1:2] + bits[0:1] + bits[2:], lambda owner: okeep[0, :, columns(owner)])
     else:
         tall_ref[:, 3 * width :] = total.T
-        outs = Reduction(u_refs, lambda owner: tall_ref[columns(owner), 3 * width :])
+        outs = Reduction(u_refs, bits[1:2] + bits[0:1] + bits[2:], lambda owner: tall_ref[columns(owner), 3 * width :])
     outs.begin()
-    others_of.middle()
-    outs.middle()
+    others_of.hold()
+    outs.hold()
+    for n in range(1, len(bits)):
+        others_of.stage(n)
+        outs.stage(n)
     for i in range(1, dp):
         count_copy(i).wait_recv()
     inverse = 1.0 / jnp.sum(tally[...], axis=0)[0:1]
@@ -589,7 +640,7 @@
     window = min(LONGEST, slots)
     heads = width // HEAD_DIM
     share, cols = slots // mp, features // dp
-    pairs, groups = mp // 2, dp // 2
+    pairs = mp // 2
     flat = cols % LANES == 0
     shapes = [(n * width, cols) if flat else (cols, n * width) for n in (2, 1, 1)]
     packed = BLOCK * mel // LANES
@@ -626,9 +677,9 @@
         bf16(pairs, width, features), bf16(pairs, width, features),
     ]
     for shape in shapes:
-        scratch += [f32(groups, *shape)] + [bf16(groups, *shape)] * 4
+        scratch += [f32(dp, *shape)] + [bf16(dp, *shape)] * 2
     scratch += [dma(dp)] * 6 + [dma(pairs, PIECES)] * 4 + [dma(pairs, 2, share)] * 4 + [dma(pairs)] * 4
-    scratch += [dma(groups)] * 12
+    scratch += [dma(dp)] * 6
     sums, out_sum = pl.pallas_call(
         functools.partial(step_kernel, dp, mp),
         out_shape=(f32(3, cols, width), f32(width, cols)),

time: 53 us -> 51.4 us (0.970)
  Pallas kernels: 52.2 us -> 50.6 us
    pallas_call x1, Pallas kernels: 51.5 us -> 49.9 us  [shards(): pl.pallas_call(functools.partial(step_kernel, dp, mp), out_shape=(f32(3,...]
where the time goes in v3:
time: 51.4 us; the launch traced here: 51.3 us
  Pallas kernels  50.6 us (98%)
  between operations  0.64 us (1%)
    pallas_call x1, Pallas kernels, shards(): pl.pallas_call(functools.partial(step_kernel, dp, mp), out_shape=(f32(3,...  49.9 us

profile of v3, /device:TPU:0, one launch (start us, length us, event | category | flops | bytes accessed | tf_op | source)
XLA Modules:
  0.0 51.3 jit_solution(1944997293890359664)
XLA Ops:
  0.6 49.9 %train_step.1 = (f32[3,128,128]{2,1,0:T(8,128)S(1)}, f32[128,128]{1,0:T(8,128)S(1)}) custom-call(s32[64]{0:T(128)} %dest_ref.1, s32[1,4]{1,0:T(1,128)} %utt_ref.1, s32[1,4]{1,0:T(1,128)} %start_ref.1, s32[1,4]{1,0:T(1,128)} %size_ref.1, s32[1,4]{1,0:T(1,128)} %step_ref.1, bf16[8,12800]{1,0:T(8,128)(2,1)} %noise_hbm.1, bf16[8,12800]{1,0:T(8,128)(2,1)} %data_hbm.1, ...), custom_call_target="tpu_custom_call" | custom-call | tf_op jit(solution)/shard_map/train_step/pallas_call | solution.py:683
  50.5 0.7 %finish.1 = (f32[3,128,128]{2,1,0:T(8,128)}, f32[128,128]{1,0:T(8,128)}) custom-call(f32[3,128,128]{2,1,0:T(8,128)S(1)} %get-tuple-element.6.a_ref, f32[128,128]{1,0:T(8,128)S(1)} %get-tuple-element.7.b_ref), custom_call_target="tpu_custom_call" | custom-call | tf_op jit(solution)/shard_map/finish/pallas_call | solution.py:696

commit v4 on v3

--- a/solution.py
+++ b/solution.py
@@ -102,7 +102,7 @@
             flat_ref[pl.ds((part * packed + r) * slots, slots)] = (
                 ref[:, r * LANES : (r + 1) * LANES].astype(F32)
             )
-    for i in range(dp):
+    def fill(i):
         to = lax.rem(me + i, dp)
         pick = jnp.int32(0)
         for k in range(slots):
@@ -117,9 +117,6 @@
         high = jnp.minimum(low + size_ref[0, u], 64)
         count += (high - low) * utt_ref[0, u] * (BLOCK // 64)
     tally[0] = jnp.full(tally.shape[1:], count, I32).astype(F32)
-    got[0] = stage[0]
-    wait()
-
     def frame_copy(i):
         return remote(
             stage.at[i, side], got.at[i, side], fsend.at[i], frecv.at[i],
@@ -135,8 +132,12 @@
         return remote(tally.at[0], tally.at[i], csend.at[i], crecv.at[i], (lax.rem(me + i, dp), my))
 
     order = sorted(range(1, dp), key=lambda i: -min(i, dp - i))
-    for i in order:
+    fill(order[0])
+    wait()
+    for n, i in enumerate(order):
         frame_copy(i).start()
+        fill(order[n + 1] if n + 1 < len(order) else 0)
+    got[0] = stage[0]
     for i in order:
         count_copy(i).start()
     loads[4].wait()

time: 51.4 us -> 51.4 us (level)
  no operation moved by 1% of the time
where the time goes in v4:
time: 51.4 us; the launch traced here: 51.3 us
  Pallas kernels  50.6 us (98%)
  between operations  0.64 us (1%)
    pallas_call x1, Pallas kernels, shards(): pl.pallas_call(functools.partial(step_kernel, dp, mp), out_shape=(f32(3,...  49.9 us

profile of v4, /device:TPU:0, one launch (start us, length us, event | category | flops | bytes accessed | tf_op | source)
XLA Modules:
  0.0 51.3 jit_solution(2918220440182553700)
XLA Ops:
  0.6 49.9 %train_step.1 = (f32[3,128,128]{2,1,0:T(8,128)S(1)}, f32[128,128]{1,0:T(8,128)S(1)}) custom-call(s32[64]{0:T(128)} %dest_ref.1, s32[1,4]{1,0:T(1,128)} %utt_ref.1, s32[1,4]{1,0:T(1,128)} %start_ref.1, s32[1,4]{1,0:T(1,128)} %size_ref.1, s32[1,4]{1,0:T(1,128)} %step_ref.1, bf16[8,12800]{1,0:T(8,128)(2,1)} %noise_hbm.1, bf16[8,12800]{1,0:T(8,128)(2,1)} %data_hbm.1, ...), custom_call_target="tpu_custom_call" | custom-call | tf_op jit(solution)/shard_map/train_step/pallas_call | solution.py:684
  50.5 0.7 %finish.1 = (f32[3,128,128]{2,1,0:T(8,128)}, f32[128,128]{1,0:T(8,128)}) custom-call(f32[3,128,128]{2,1,0:T(8,128)S(1)} %get-tuple-element.6.a_ref, f32[128,128]{1,0:T(8,128)S(1)} %get-tuple-element.7.b_ref), custom_call_target="tpu_custom_call" | custom-call | tf_op jit(solution)/shard_map/finish/pallas_call | solution.py:697
